TPU v7x, 32 devices: a whole 2x2x4 slice. The times are simulated.
32 devices in a mesh: dom: 8 (over z, y), edge: 4 (over x, core).
Axes of the slice: x: 2, y: 2, z: 4, core: 2. Of those that a mesh axis runs over, the one named last changes fastest.
Arguments:
- embeddings: float32 [4096, 400], P(('dom', 'edge')), may hold values from -1.2 to 1.2
- adagrad_state: float32 [4096], P(('dom', 'edge')), may hold values from 0.01 to 1
- relations: bfloat16 [256, 400], replicated, may hold values from -4 to 4
- endpoints: int32 [2, 2, 8, 2048], P(None, None, 'dom', 'edge'), may hold values from 0 to 511
- relation_ids: int32 [2, 8, 2048], P(None, 'dom', 'edge'), may hold values from 0 to 255
- negatives: int32 [2, 2, 8, 8, 256], P(None, None, 'dom', 'edge'), may hold values from 0 to 511
- edge_counts: int32 [2, 8, 4], P(None, 'dom', 'edge'), may hold values from 1 to 512, as said below
- plan: int32 [2], replicated, may hold values from 1 to 7, as said below
Outputs:
- new_embeddings: float32 [4096, 400], P(('dom', 'edge'))
- new_state: float32 [4096], P(('dom', 'edge'))
Inputs may be any that keep to these rules, and one draw needn't show every extreme that they name: `edge_counts`: in every round some edge group has all 512 slots live; live slots come first. `plan`: consecutive rounds have different patterns; some round has the pattern 8 - 1.
All inputs are finite; a program needn't handle non-finite values.
Results may differ from a plain program's by a relative error of at most 0.01.
Values may be sent and summed in bfloat16 or wider, within the bound.
No kernel may reach another device: no remote copies, remote signals or barrier semaphores. Data moves between devices by JAX's collectives and lax.ppermute only.
A program may use at most 64 MiB of HBM per device.

v0:
```python
import functools

import jax
import jax.numpy as jnp
from jax import lax
from jax.experimental import pallas as pl
from jax.experimental.pallas import tpu as pltpu
from jax.sharding import PartitionSpec as P


learning_rate = 0.2
AXES = ("dom", "edge")
CHUNK_BITS = 3
VMEM = pl.BlockSpec(memory_space=pltpu.VMEM)
f32, bf16 = jnp.float32, jnp.bfloat16


def exchange(value, dom_mask, edge_mask):
    doms, edges = lax.axis_size("dom"), lax.axis_size("edge")
    pairs = [
        (d * edges + e, (d ^ dom_mask) * edges + (e ^ edge_mask))
        for d in range(doms)
        for e in range(edges)
    ]
    return lax.ppermute(value, AXES, pairs)


def chunks():
    bits = lax.axis_size("dom").bit_length() - 1
    return [(low, min(CHUNK_BITS, bits - low)) for low in range(0, bits, CHUNK_BITS)]


def walked(values, mask):
    for low, bits in chunks()[:-1]:
        field = jnp.right_shift(mask, low) & (2**bits - 1)
        branches = [
            (lambda *v, m=m: tuple(exchange(a, m << low, 0) for a in v) if m else v)
            for m in range(2**bits)
        ]
        values = lax.switch(field, branches, *values)
    return values


def last_run():
    runs = chunks()
    return (*runs[-1], 1 if len(runs) == 1 else 0)


def switched(field, branch, *values):
    low, bits, first = last_run()
    branches = [(lambda *v, m=m: branch(m << low, *v)) for m in range(first, 2**bits)]
    return lax.switch(field.reshape(()), branches, *values)


def piece(table, index, rows):
    return table[:, index * rows : (index + 1) * rows]


def gathered(block, mask, field):
    def branch(dom_mask, block, moved):
        near = exchange(moved, dom_mask, 0) if dom_mask else moved
        far = exchange(moved, dom_mask, 2)
        cross = exchange(block, 0, 2)
        return jnp.concatenate([block, cross, near, far], axis=1)

    (moved,) = walked((block,), mask)
    return switched(field, branch, block, moved)


def returned(near, far, sent, kept, mask, field):
    near, far = walked((near, far), mask) if len(chunks()) > 1 else (near, far)
    rows = near.shape[1]

    def branch(dom_mask, near, far, sent, kept):
        beside = exchange(sent, 0, 1)
        sums = kept.astype(f32) + beside.astype(f32)
        near = exchange(near, dom_mask, 0) if dom_mask else near
        far = exchange(far, dom_mask, 2)
        cross = exchange(piece(sums, 1, rows).astype(bf16), 0, 2)
        return far.astype(f32) + near.astype(f32) + (cross.astype(f32) + piece(sums, 0, rows))

    return switched(field, branch, near, far, sent, kept)


def dot(a, b):
    return jnp.dot(a, b, preferred_element_type=f32)


def dot_nt(a, b):
    return lax.dot_general(a, b, (((1,), (1,)), ((), ())), preferred_element_type=f32)


def dot_tn(a, b):
    return lax.dot_general(a, b, (((0,), (0,)), ((), ())), preferred_element_type=f32)


def product(left, right):
    half = left.shape[0] // 2
    a, b, c, d = left[:half], left[half:], right[:half], right[half:]
    return jnp.concatenate([a * c - b * d, a * d + b * c], axis=0)


def conjugate(values):
    half = values.shape[0] // 2
    return jnp.concatenate([values[:half], -values[half:]], axis=0)


def sigmoid(x):
    return 0.5 * jnp.tanh(0.5 * x) + 0.5


def prepare_kernel(
    round_index,
    held,
    relations,
    ends,
    rels,
    negs,
    state,
    hot_lhs,
    hot_rhs,
    rel,
    part_lhs,
    part_rhs,
    state_out,
):
    state_out[...] = state[...]
    r = round_index
    half = held.shape[1] // 2
    rows = half // 2
    blocks, count = negs.shape[3], negs.shape[4]
    edges = ends.shape[3]
    me = lax.axis_index("edge")

    def place(ids):
        slot = jnp.right_shift(ids, rows.bit_length() - 1) ^ me
        slot = jnp.right_shift(slot, 1) | ((slot & 1) << 1)
        return (slot << (rows.bit_length() - 1)) | (ids & (rows - 1))

    def hot(ids, n):
        return (lax.broadcasted_iota(jnp.int32, (n, ids.shape[1]), 0) == ids).astype(f32).astype(bf16)

    for side, hots in ((0, hot_lhs), (1, hot_rhs)):
        hots[:, :edges] = hot(place(ends[r, side]), 2 * half)
        for c in range(blocks):
            columns = slice(edges + c * count, edges + (c + 1) * count)
            hots[:, columns] = hot(place(negs[r, side, 0, c : c + 1]), 2 * half)
    hot_rel = hot(rels[r], relations.shape[1])
    rel[...] = dot(relations[...], hot_rel).astype(bf16)
    part_lhs[...] = dot(held[:, :half], hot_lhs[:half]).astype(bf16)
    part_rhs[...] = dot(held[:, half:], hot_rhs[:half]).astype(bf16)


def bucket_kernel(
    round_index,
    blocks,
    came,
    hot_lhs,
    hot_rhs,
    rel_ref,
    part_lhs,
    part_rhs,
    counts,
    sent,
    kept,
    grad_lhs,
    grad_rhs,
    rows_lhs,
    rows_rhs,
    query_ref,
    back_ref,
    weight_rhs_ref,
    weight_lhs_ref,
):
    half = came.shape[1] // 2
    edges = rel_ref.shape[1]
    size = edges // blocks
    negs = (hot_lhs.shape[1] - edges) // blocks
    limit = counts[round_index]
    at = [slice(c * size, (c + 1) * size) for c in range(blocks)]
    drawn = [slice(edges + c * negs, edges + (c + 1) * negs) for c in range(blocks)]

    def gather(columns):
        rows_lhs[:, columns] = part_lhs[:, columns] + dot(came[:, :half], hot_lhs[half:, columns]).astype(bf16)
        rows_rhs[:, columns] = part_rhs[:, columns] + dot(came[:, half:], hot_rhs[half:, columns]).astype(bf16)

    def products(c):
        rel = rel_ref[:, at[c]].astype(f32)
        query_ref[:, at[c]] = product(rows_lhs[:, at[c]].astype(f32), rel).astype(bf16)
        back_ref[:, at[c]] = product(conjugate(rel), rows_rhs[:, at[c]].astype(f32)).astype(bf16)

    def weights(c):
        scale = jnp.where(
            lax.broadcasted_iota(jnp.int32, (size, 1), 0) + c * size < limit, 0.25 / negs, 0.0
        )
        for ref, edge_rows, rows in (
            (weight_rhs_ref, query_ref, rows_rhs),
            (weight_lhs_ref, back_ref, rows_lhs),
        ):
            scores = dot_tn(edge_rows[:, at[c]], rows[:, drawn[c]])
            ref[at[c]] = (jnp.tanh(0.5 * scores) * scale + scale).astype(bf16)

    def grads(c):
        rel = rel_ref[:, at[c]].astype(f32)
        query = query_ref[:, at[c]].astype(f32)
        rhs = rows_rhs[:, at[c]].astype(f32)
        positive = jnp.sum(query * rhs, axis=0, keepdims=True)
        live = lax.broadcasted_iota(jnp.int32, (1, size), 1) + c * size < limit
        weight_pos = jnp.where(live, -sigmoid(-positive), 0.0)
        grad_query = weight_pos * rhs + dot_nt(rows_rhs[:, drawn[c]], weight_rhs_ref[at[c]])
        grad_back = dot_nt(rows_lhs[:, drawn[c]], weight_lhs_ref[at[c]])
        grad_lhs[:, at[c]] = product(grad_query, conjugate(rel)).astype(bf16)
        grad_rhs[:, at[c]] = (weight_pos * query + product(grad_back, rel)).astype(bf16)
        grad_rhs[:, drawn[c]] = dot(query_ref[:, at[c]], weight_rhs_ref[at[c]]).astype(bf16)
        grad_lhs[:, drawn[c]] = dot(back_ref[:, at[c]], weight_lhs_ref[at[c]]).astype(bf16)

    for c in range(blocks + 2):
        if c < blocks:
            gather(at[c])
            gather(drawn[c])
            products(c)
        if 1 <= c <= blocks:
            weights(c - 1)
        if c >= 2:
            grads(c - 2)
    sent[...] = dot_nt(grad_rhs[...], hot_rhs[half:]).astype(bf16)
    kept[...] = dot_nt(grad_rhs[...], hot_rhs[:half]).astype(bf16)


def own_kernel(grad_lhs, hot_lhs, sent, kept):
    half = sent.shape[1]
    sent[...] = dot_nt(grad_lhs[...], hot_lhs[half:]).astype(bf16)
    kept[...] = dot_nt(grad_lhs[...], hot_lhs[:half]).astype(bf16)


def start_kernel(low, bits, first, rows, plan, block, *rest):
    *fields, rows_here, plan_here, fields_here, in_sems, out_sems = rest
    plan_copy = pltpu.make_async_copy(plan, plan_here, in_sems.at[0])
    rows_copy = pltpu.make_async_copy(rows, rows_here, in_sems.at[1])
    plan_copy.start()
    rows_copy.start()
    plan_copy.wait()
    outs = []
    for r, field in enumerate(fields):
        fields_here[r, 0] = (jnp.right_shift(plan_here[r], low) & (2**bits - 1)) - first
        outs.append(pltpu.make_async_copy(fields_here.at[r], field, out_sems.at[r]))
        outs[-1].start()
    rows_copy.wait()
    block[...] = rows_here[...].astype(bf16)
    for copy in outs:
        copy.wait()


def update_kernel(total, rows, state, rows_out, state_out, *block):
    grad = total[...]
    sums = state[...] + jnp.mean(grad * grad, axis=0, keepdims=True)
    new = rows[...] - learning_rate * grad / jnp.sqrt(sums)
    state_out[...] = sums
    rows_out[...] = new
    for b in block:
        b[...] = new.astype(bf16)


def call(kernel, outs, args, flops, scratch=(), in_specs=None, out_specs=None, grant=32):
    return pl.pallas_call(
        kernel,
        out_shape=[jax.ShapeDtypeStruct(*out) for out in outs],
        in_specs=in_specs or [VMEM] * len(args),
        out_specs=out_specs or [VMEM] * len(outs),
        scratch_shapes=list(scratch),
        compiler_params=pltpu.CompilerParams(vmem_limit_bytes=grant * 2**20),
        cost_estimate=pl.CostEstimate(flops=flops, bytes_accessed=2**20, transcendentals=0),
    )(*args)


def on_device(
    embeddings, adagrad_state, relations, endpoints, relation_ids, negatives, edge_counts, plan
):
    rows, width = embeddings.shape
    edges = endpoints.shape[3]
    blocks, negs = negatives.shape[3:]
    part_rows = rows * lax.axis_size("edge")
    drawn = edges + blocks * negs
    relations = relations.T
    rounds = plan.shape[0]
    whole, column = ((width, rows), f32), ((1, rows), f32)
    anywhere = pl.BlockSpec(memory_space=pltpu.HBM)
    table, state = embeddings.T, adagrad_state[None, :]
    block, *fields = call(
        functools.partial(start_kernel, *last_run()),
        [((width, rows), bf16)] + [((1,), jnp.int32)] * rounds,
        (table, plan),
        1000,
        [
            pltpu.VMEM((width, rows), f32),
            pltpu.SMEM((rounds,), jnp.int32),
            pltpu.SMEM((rounds, 1), jnp.int32),
            pltpu.SemaphoreType.DMA((2,)),
            pltpu.SemaphoreType.DMA((rounds,)),
        ],
        in_specs=[anywhere] * 2,
        out_specs=[VMEM] + [anywhere] * rounds,
        grant=63,
    )
    for round_index in range(rounds):
        mask, field = plan[round_index], fields[round_index]
        held = gathered(block, mask, field)
        came = exchange(held, 0, 1)
        *prepared, state = call(
            functools.partial(prepare_kernel, round_index),
            [((part_rows, drawn), bf16)] * 2 + [((width, edges), bf16)] + [((width, drawn), bf16)] * 2 + [column],
            (held, relations, endpoints, relation_ids, negatives, state),
            2 * width * (drawn * part_rows + edges * relations.shape[1]),
        )
        pair = [((width, part_rows // 2), bf16)] * 2
        sent, kept, grads = call(
            functools.partial(bucket_kernel, round_index, blocks),
            pair + [((width, drawn), bf16)],
            (came, *prepared, edge_counts),
            2 * width * drawn * 3 * part_rows,
            [pltpu.VMEM((width, drawn), bf16)] * 3
            + [pltpu.VMEM((width, edges), bf16)] * 2
            + [pltpu.VMEM((edges, negs), bf16)] * 2,
        )
        came = exchange(sent, 0, 1)
        sent_own, kept_own = call(own_kernel, pair, (grads, prepared[0]), 2 * width * drawn * part_rows)
        sums = kept.astype(f32) + came.astype(f32)
        near, far = (piece(sums, i, rows).astype(bf16) for i in range(2))
        total = returned(near, far, sent_own, kept_own, mask, field)
        last = round_index == rounds - 1
        table, state, *block = call(
            update_kernel,
            [whole, column] + ([] if last else [((width, rows), bf16)]),
            (total, table, state),
            1000,
            out_specs=[pl.BlockSpec()] * 2 if last else None,
        )
        block = block[0] if block else None
    return (table.T, state[0])


def solution(mesh):
    in_specs = (
        P(("dom", "edge"), None),
        P(("dom", "edge")),
        P(),
        P(None, None, "dom", "edge"),
        P(None, "dom", "edge"),
        P(None, None, "dom", "edge", None),
        P(None, "dom", "edge"),
        P(),
    )
    out_specs = (P(("dom", "edge"), None), P(("dom", "edge")))
    return jax.shard_map(
        on_device, mesh=mesh, in_specs=in_specs, out_specs=out_specs, check_vma=False
    )
```

profile of v0, /device:TPU:0, one launch (start us, length us, event | category | flops | bytes accessed | tf_op | source)
XLA Modules:
  0.0 67.9 jit_solution(2460504296564964462)
XLA Ops:
  0.6 1.2 %shard_map.95 = (bf16[400,128]{1,0:T(8,128)(2,1)S(1)}, s32[1]{0:T(128)}, s32[1]{0:T(128)}) custom-call(f32[400,128]{1,0:T(8,128)} %bitcast.7, s32[2]{0:T(128)} %plan.1), custom_call_target="tpu_custom_call" | custom-call | flops 1000 | bytes 1048576 | tf_op jit(solution)/shard_map/pallas_call | solution.py:265
  2.5 0.0 copy-start.2
  2.5 0.0 copy-start.3
  2.6 14.5 %conditional.4 = (bf16[400,512]{1,0:T(8,128)(2,1)S(1)}) conditional(s32[]{:T(128)} %bitcast.2, bf16[400,128]{1,0:T(8,128)(2,1)S(1)} %get-tuple-element.248, bf16[400,128]{1,0:T(8,128)(2,1)S(1)} %get-tuple-element.248, bf16[400,128]{1,0:T(8,128)(2,1)S(1)} %get-tuple-element.248, ...), branch_computations={%region_0.0_spmd, %region_1.0_spmd, %region_2.0_spmd, %region_3.0_... | conditional | flops 1638400 | bytes 2048128 | solution.py:52
  2.6 7.0 %collective-permute-start.20 = (bf16[400,128]{1,0:T(8,128)(2,1)S(1)}, bf16[400,128]{1,0:T(8,128)(2,1)S(1)}, u32[]{:S(2)}, u32[]{:S(2)}) collective-permute-start(bf16[400,128]{1,0:T(8,128)(2,1)S(1)} %param.6), channel_id=1, source_target_pairs={{0,30},{1,31},{2,28},{3,29},{4,26},{5,27},{6,24},{7,25},{8,22},{9,... | collective-permute-start | bytes 307208 | tf_op jit(solution)/shard_map/cond/branch_6_fun/ppermute | solution.py:25
  9.6 0.2 collective-permute-start.19
  9.8 0.5 collective-permute-start.18
  10.3 2.6 %collective-permute-done.20 = bf16[400,128]{1,0:T(8,128)(2,1)S(1)} collective-permute-done((bf16[400,128]{1,0:T(8,128)(2,1)S(1)}, bf16[400,128]{1,0:T(8,128)(2,1)S(1)}, u32[]{:S(2)}, u32[]{:S(2)}) %collective-permute-start.20) | collective-permute-done | bytes 102432 | tf_op jit(solution)/shard_map/cond/branch_6_fun/ppermute | solution.py:25
  12.9 4.1 %collective-permute-done.19 = bf16[400,128]{1,0:T(8,128)(2,1)S(1)} collective-permute-done((bf16[400,128]{1,0:T(8,128)(2,1)S(1)}, bf16[400,128]{1,0:T(8,128)(2,1)S(1)}, u32[]{:S(2)}, u32[]{:S(2)}) %collective-permute-start.19) | collective-permute-done | bytes 102432 | tf_op jit(solution)/shard_map/cond/branch_6_fun/ppermute | solution.py:25
  17.1 0.1 collective-permute-start.98
  17.1 0.1 copy.10.counts
  17.3 0.5 copy-done.4
  17.7 0.2 copy-done.5
  17.9 1.1 %shard_map.96 = (bf16[512,1024]{1,0:T(8,128)(2,1)S(1)}, bf16[512,1024]{1,0:T(8,128)(2,1)S(1)}, bf16[400,512]{1,0:T(8,128)(2,1)S(1)}, bf16[400,1024]{1,0:T(8,128)...) custom-call(bf16[400,512]{1,0:T(8,128)(2,1)S(1)} %get-tuple-element.280.held, ...), custom_call_target="tpu_custom_call" | custom-call | flops 524288000 | bytes 1048576 | tf_op jit(solution)/shard_map/pallas_call | solution.py:265
  19.0 2.4 %shard_map.97 = (bf16[400,256]{1,0:T(8,128)(2,1)S(1)}, bf16[400,256]{1,0:T(8,128)(2,1)S(1)}, bf16[400,1024]{1,0:T(8,128)(2,1)S(1)}) custom-call(bf16[400,512]{1,0:T(8,128)(2,1)S(1)} %collective-permute-done.98.came, bf16[512,1024]{1,0:T(8,128)(2,1)S(1)} %get-tuple-element.249.hot_lhs, bf16[512,1024]{1,0:T(8,128)(2,1)S(1)} %get-tuple-element.250.hot_rhs, ...), custom_call_target="tpu_custom_call" | custom-call | flops 1258291200 | bytes 1048576 | tf_op jit(solution)/shard_map/pallas_call | solution.py:265
  21.3 0.6 collective-permute-start.99
  22.6 0.6 shard_map.98
  23.2 0.1 add_convert_fusion.1
  23.3 11.5 %conditional.5 = (f32[400,128]{1,0:T(8,128)S(1)}) conditional(s32[]{:T(128)} %bitcast.2, (bf16[400,128]{1,0:T(8,128)(2,1)S(1)}, bf16[400,128]{1,0:T(8,128)(2,1)S(1)}, bf16[400,256]{1,0:T(8,128)(2,1)S(1)}, bf16[400,256]{1,0:T(8,128)(2,1)S(1)}) %tuple.92, (bf16[400,128]{1,0:T(8,128)(2,1)S(1)}, ...), branch_computations={%region_7.0_spmd, %region_8.0_spmd, %region_9.0_spmd, %region_10.0... | conditional | flops 614400 | bytes 3788968 | solution.py:52
  23.3 0.2 collective-permute-start.47
  23.6 3.2 %collective-permute-start.45 = (bf16[400,128]{1,0:T(8,128)(2,1)S(1)}, bf16[400,128]{1,0:T(8,128)(2,1)S(1)}, u32[]{:S(2)}, u32[]{:S(2)}) collective-permute-start(bf16[400,128]{1,0:T(8,128)(2,1)S(1)} %get-tuple-element.182), channel_id=1, source_target_pairs={{0,30},{1,31},{2,28},{3,29},{4,26},{5,27},{6,24},{7,25},{8,22},{9,... | collective-permute-start | bytes 307208 | tf_op jit(solution)/shard_map/cond/branch_6_fun/ppermute | solution.py:25
  26.7 1.5 %collective-permute-start.46 = (bf16[400,128]{1,0:T(8,128)(2,1)S(1)}, bf16[400,128]{1,0:T(8,128)(2,1)S(1)}, u32[]{:S(2)}, u32[]{:S(2)}) collective-permute-start(bf16[400,128]{1,0:T(8,128)(2,1)S(1)} %get-tuple-element.183), channel_id=1, source_target_pairs={{0,28},{1,29},{2,30},{3,31},{4,24},{5,25},{6,26},{7,27},{8,20},{9,... | collective-permute-start | bytes 307208 | tf_op jit(solution)/shard_map/cond/branch_6_fun/ppermute | solution.py:25
  28.3 1.6 %collective-permute-start.48 = (bf16[400,128]{1,0:T(8,128)(2,1)S(1)}, bf16[400,128]{1,0:T(8,128)(2,1)S(1)}, u32[]{:S(2)}, u32[]{:S(2)}) collective-permute-start(bf16[400,128]{1,0:T(8,128)(2,1)S(1)} %slice.212), channel_id=1, source_target_pairs={{0,2},{1,3},{2,0},{3,1},{4,6},{5,7},{6,4},{7,5},{8,10},{9,11},{10,... | collective-permute-start | bytes 307208 | tf_op jit(solution)/shard_map/cond/branch_6_fun/ppermute | solution.py:25
  29.9 3.1 %collective-permute-done.45 = bf16[400,128]{1,0:T(8,128)(2,1)S(1)} collective-permute-done((bf16[400,128]{1,0:T(8,128)(2,1)S(1)}, bf16[400,128]{1,0:T(8,128)(2,1)S(1)}, u32[]{:S(2)}, u32[]{:S(2)}) %collective-permute-start.45) | collective-permute-done | bytes 102432 | tf_op jit(solution)/shard_map/cond/branch_6_fun/ppermute | solution.py:25
  33.0 1.7 %collective-permute-done.46 = bf16[400,128]{1,0:T(8,128)(2,1)S(1)} collective-permute-done((bf16[400,128]{1,0:T(8,128)(2,1)S(1)}, bf16[400,128]{1,0:T(8,128)(2,1)S(1)}, u32[]{:S(2)}, u32[]{:S(2)}) %collective-permute-start.46) | collective-permute-done | bytes 102432 | tf_op jit(solution)/shard_map/cond/branch_6_fun/ppermute | solution.py:25
  34.7 0.1 fusion.6
  34.8 0.1 shard_map.99
  34.9 14.7 %conditional.6 = (bf16[400,512]{1,0:T(8,128)(2,1)S(1)}) conditional(s32[]{:T(128)} %bitcast.1, bf16[400,128]{1,0:T(8,128)(2,1)S(1)} %get-tuple-element.260, bf16[400,128]{1,0:T(8,128)(2,1)S(1)} %get-tuple-element.260, bf16[400,128]{1,0:T(8,128)(2,1)S(1)} %get-tuple-element.260, ...), branch_computations={%region_14.0_spmd, %region_15.0_spmd, %region_16.0_spmd, %region_1... | conditional | flops 1638400 | bytes 2048128 | solution.py:52
  34.9 5.6 %collective-permute-start.60 = (bf16[400,128]{1,0:T(8,128)(2,1)S(1)}, bf16[400,128]{1,0:T(8,128)(2,1)S(1)}, u32[]{:S(2)}, u32[]{:S(2)}) collective-permute-start(bf16[400,128]{1,0:T(8,128)(2,1)S(1)} %param.17), channel_id=1, source_target_pairs={{0,18},{1,19},{2,16},{3,17},{4,22},{5,23},{6,20},{7,21},{8,26},{9,... | collective-permute-start | bytes 307208 | tf_op jit(solution)/shard_map/cond/branch_3_fun/ppermute | solution.py:25
  40.5 0.7 collective-permute-start.58
  41.2 7.5 %collective-permute-done.60 = bf16[400,128]{1,0:T(8,128)(2,1)S(1)} collective-permute-done((bf16[400,128]{1,0:T(8,128)(2,1)S(1)}, bf16[400,128]{1,0:T(8,128)(2,1)S(1)}, u32[]{:S(2)}, u32[]{:S(2)}) %collective-permute-start.60) | collective-permute-done | bytes 102432 | tf_op jit(solution)/shard_map/cond/branch_3_fun/ppermute | solution.py:25
  48.6 0.7 %collective-permute-done.59 = bf16[400,128]{1,0:T(8,128)(2,1)S(1)} collective-permute-done((bf16[400,128]{1,0:T(8,128)(2,1)S(1)}, bf16[400,128]{1,0:T(8,128)(2,1)S(1)}, u32[]{:S(2)}, u32[]{:S(2)}) %collective-permute-start.59) | collective-permute-done | bytes 102432 | tf_op jit(solution)/shard_map/cond/branch_3_fun/ppermute | solution.py:25
  49.6 0.1 collective-permute-start.100
  49.7 1.1 %shard_map.100 = (bf16[512,1024]{1,0:T(8,128)(2,1)S(1)}, bf16[512,1024]{1,0:T(8,128)(2,1)S(1)}, bf16[400,512]{1,0:T(8,128)(2,1)S(1)}, bf16[400,1024]{1,0:T(8,128...) custom-call(bf16[400,512]{1,0:T(8,128)(2,1)S(1)} %get-tuple-element.282.held, ...), custom_call_target="tpu_custom_call" | custom-call | flops 524288000 | bytes 1048576 | tf_op jit(solution)/shard_map/pallas_call | solution.py:265
  50.7 0.7 collective-permute-done.100.came
  51.4 2.3 %shard_map.101 = (bf16[400,256]{1,0:T(8,128)(2,1)S(1)}, bf16[400,256]{1,0:T(8,128)(2,1)S(1)}, bf16[400,1024]{1,0:T(8,128)(2,1)S(1)}) custom-call(bf16[400,512]{1,0:T(8,128)(2,1)S(1)} %collective-permute-done.100.came, bf16[512,1024]{1,0:T(8,128)(2,1)S(1)} %get-tuple-element.262.hot_lhs, bf16[512,1024]{1,0:T(8,128)(2,1)S(1)} %get-tuple-element.263.hot_rhs, ...), custom_call_target="tpu_custom_call" | custom-call | flops 1258291200 | bytes 1048576 | tf_op jit(solution)/shard_map/pallas_call | solution.py:265
  53.7 0.2 collective-permute-start.101
  53.9 0.6 shard_map.102
  54.6 0.7 %collective-permute-done.101 = bf16[400,256]{1,0:T(8,128)(2,1)S(1)} collective-permute-done((bf16[400,256]{1,0:T(8,128)(2,1)S(1)}, bf16[400,256]{1,0:T(8,128)(2,1)S(1)}, u32[]{:S(2)}, u32[]{:S(2)}) %collective-permute-start.101) | collective-permute-done | bytes 204832 | tf_op jit(solution)/shard_map/ppermute | solution.py:25
  55.3 11.8 %conditional.7 = (f32[400,128]{1,0:T(8,128)S(1)}) conditional(s32[]{:T(128)} %bitcast.1, (bf16[400,128]{1,0:T(8,128)(2,1)S(1)}, bf16[400,128]{1,0:T(8,128)(2,1)S(1)}, bf16[400,256]{1,0:T(8,128)(2,1)S(1)}, bf16[400,256]{1,0:T(8,128)(2,1)S(1)}) %tuple.93, (bf16[400,128]{1,0:T(8,128)(2,1)S(1)}, ...), branch_computations={%region_21.0_spmd, %region_22.0_spmd, %region_23.0_spmd, %region_2... | conditional | flops 614400 | bytes 3788968 | solution.py:52
  55.4 0.2 collective-permute-start.84
  55.6 0.4 collective-permute-start.82
  55.9 3.4 %collective-permute-start.83 = (bf16[400,128]{1,0:T(8,128)(2,1)S(1)}, bf16[400,128]{1,0:T(8,128)(2,1)S(1)}, u32[]{:S(2)}, u32[]{:S(2)}) collective-permute-start(bf16[400,128]{1,0:T(8,128)(2,1)S(1)} %get-tuple-element.199), channel_id=1, source_target_pairs={{0,16},{1,17},{2,18},{3,19},{4,20},{5,21},{6,22},{7,23},{8,24},{9,... | collective-permute-start | bytes 307208 | tf_op jit(solution)/shard_map/cond/branch_3_fun/ppermute | solution.py:25
  59.4 0.7 %collective-permute-start.85 = (bf16[400,128]{1,0:T(8,128)(2,1)S(1)}, bf16[400,128]{1,0:T(8,128)(2,1)S(1)}, u32[]{:S(2)}, u32[]{:S(2)}) collective-permute-start(bf16[400,128]{1,0:T(8,128)(2,1)S(1)} %slice.216), channel_id=1, source_target_pairs={{0,2},{1,3},{2,0},{3,1},{4,6},{5,7},{6,4},{7,5},{8,10},{9,11},{10,... | collective-permute-start | bytes 307208 | tf_op jit(solution)/shard_map/cond/branch_3_fun/ppermute | solution.py:25
  60.1 5.4 %collective-permute-done.82 = bf16[400,128]{1,0:T(8,128)(2,1)S(1)} collective-permute-done((bf16[400,128]{1,0:T(8,128)(2,1)S(1)}, bf16[400,128]{1,0:T(8,128)(2,1)S(1)}, u32[]{:S(2)}, u32[]{:S(2)}) %collective-permute-start.82) | collective-permute-done | bytes 102432 | tf_op jit(solution)/shard_map/cond/branch_3_fun/ppermute | solution.py:25
  65.5 1.5 %collective-permute-done.83 = bf16[400,128]{1,0:T(8,128)(2,1)S(1)} collective-permute-done((bf16[400,128]{1,0:T(8,128)(2,1)S(1)}, bf16[400,128]{1,0:T(8,128)(2,1)S(1)}, u32[]{:S(2)}, u32[]{:S(2)}) %collective-permute-start.83) | collective-permute-done | bytes 102432 | tf_op jit(solution)/shard_map/cond/branch_3_fun/ppermute | solution.py:25
  67.0 0.1 fusion.10
  67.1 0.8 %shard_map.103 = (f32[400,128]{1,0:T(8,128)}, f32[1,128]{1,0:T(1,128)}) custom-call(f32[400,128]{1,0:T(8,128)S(1)} %get-tuple-element.283.total, f32[400,128]{1,0:T(8,128)S(1)} %get-tuple-element.272.rows, f32[1,128]{1,0:T(1,128)S(1)} %get-tuple-element.273.state), custom_call_target="tpu_custom_call" | custom-call | flops 1000 | bytes 1048576 | tf_op jit(solution)/shard_map/pallas_call | solution.py:265
  (28 shorter events, 0.4 us)
Async XLA Ops:
  2.5 14.6 %copy-start.6 = (s32[2,1,1]{0,2,1:T(1,128)S(1)}, s32[2,1,1]{0,2,1:T(1,128)}, u32[]{:S(2)}) copy-start(s32[2,1,1]{0,2,1:T(1,128)} %param.42) | copy-start | bytes 28
  2.5 14.7 %copy-start.1 = (bf16[256,400]{0,1:T(8,128)(2,1)S(1)}, bf16[256,400]{0,1:T(8,128)(2,1)}, u32[]{:S(2)}) copy-start(bf16[256,400]{0,1:T(8,128)(2,1)} %param.38) | copy-start | bytes 614404
  2.5 14.7 %copy-start.2 = (s32[2,2,1,512]{3,2,1,0:T(1,128)S(1)}, s32[2,2,1,512]{3,2,1,0:T(1,128)}, u32[]{:S(2)}) copy-start(s32[2,2,1,512]{3,2,1,0:T(1,128)} %ends.3) | copy-start | bytes 24580
  2.5 14.7 %copy-start.3 = (s32[2,2,1,2,256]{4,3,2,1,0:T(2,128)S(1)}, s32[2,2,1,2,256]{4,3,2,1,0:T(2,128)}, u32[]{:S(2)}) copy-start(s32[2,2,1,2,256]{4,3,2,1,0:T(2,128)} %negs.3) | copy-start | bytes 24580
  2.6 10.3 %collective-permute-start.20 = (bf16[400,128]{1,0:T(8,128)(2,1)S(1)}, bf16[400,128]{1,0:T(8,128)(2,1)S(1)}, u32[]{:S(2)}, u32[]{:S(2)}) collective-permute-start(bf16[400,128]{1,0:T(8,128)(2,1)S(1)} %param.6), channel_id=1, source_target_pairs={{0,30},{1,31},{2,28},{3,29},{4,26},{5,27},{6,24},{7,25},{8,22},{9,... | collective-permute-start | bytes 307208 | tf_op jit(solution)/shard_map/cond/branch_6_fun/ppermute | solution.py:25
  9.6 7.4 %collective-permute-start.19 = (bf16[400,128]{1,0:T(8,128)(2,1)S(1)}, bf16[400,128]{1,0:T(8,128)(2,1)S(1)}, u32[]{:S(2)}, u32[]{:S(2)}) collective-permute-start(bf16[400,128]{1,0:T(8,128)(2,1)S(1)} %param.6), channel_id=1, source_target_pairs={{0,28},{1,29},{2,30},{3,31},{4,24},{5,25},{6,26},{7,27},{8,20},{9,... | collective-permute-start | bytes 307208 | tf_op jit(solution)/shard_map/cond/branch_6_fun/ppermute | solution.py:25
  9.8 7.2 %collective-permute-start.18 = (bf16[400,128]{1,0:T(8,128)(2,1)S(1)}, bf16[400,128]{1,0:T(8,128)(2,1)S(1)}, u32[]{:S(2)}, u32[]{:S(2)}) collective-permute-start(bf16[400,128]{1,0:T(8,128)(2,1)S(1)} %param.6), channel_id=1, source_target_pairs={{0,2},{1,3},{2,0},{3,1},{4,6},{5,7},{6,4},{7,5},{8,10},{9,11},{10,... | collective-permute-start | bytes 307208 | tf_op jit(solution)/shard_map/cond/branch_6_fun/ppermute | solution.py:25
  17.0 0.7 %copy-start.4 = (s32[2,1,512]{2,1,0:T(1,128)S(1)}, s32[2,1,512]{2,1,0:T(1,128)}, u32[]{:S(2)}) copy-start(s32[2,1,512]{2,1,0:T(1,128)} %rels.3) | copy-start | bytes 12292
  17.1 1.9 %collective-permute-start.98 = (bf16[400,512]{1,0:T(8,128)(2,1)S(1)}, bf16[400,512]{1,0:T(8,128)(2,1)S(1)}, u32[]{:S(2)}, u32[]{:S(2)}) collective-permute-start(bf16[400,512]{1,0:T(8,128)(2,1)S(1)} %get-tuple-element.280.held), channel_id=1, source_target_pairs={{0,1},{1,0},{2,3},{3,2},{4,5},{5,4},{6,7},{7,6},{8,9},{9,8},{10,11... | collective-permute-start | bytes 1228808 | tf_op jit(solution)/shard_map/ppermute | solution.py:25
  17.2 0.7 copy-start.5
  21.3 1.8 %collective-permute-start.99 = (bf16[400,256]{1,0:T(8,128)(2,1)S(1)}, bf16[400,256]{1,0:T(8,128)(2,1)S(1)}, u32[]{:S(2)}, u32[]{:S(2)}) collective-permute-start(bf16[400,256]{1,0:T(8,128)(2,1)S(1)} %get-tuple-element.255), channel_id=1, source_target_pairs={{0,1},{1,0},{2,3},{3,2},{4,5},{5,4},{6,7},{7,6},{8,9},{9,8},{10,11... | collective-permute-start | bytes 614408 | tf_op jit(solution)/shard_map/ppermute | solution.py:25
  23.3 11.5 %copy-start = (f32[128,400]{0,1:T(8,128)S(1)}, f32[128,400]{0,1:T(8,128)}, u32[]{:S(2)}) copy-start(f32[128,400]{0,1:T(8,128)} %param.36) | copy-start | bytes 614404
  23.3 4.9 %collective-permute-start.47 = (bf16[400,256]{1,0:T(8,128)(2,1)S(1)}, bf16[400,256]{1,0:T(8,128)(2,1)S(1)}, u32[]{:S(2)}, u32[]{:S(2)}) collective-permute-start(bf16[400,256]{1,0:T(8,128)(2,1)S(1)} %get-tuple-element.185), channel_id=1, source_target_pairs={{0,1},{1,0},{2,3},{3,2},{4,5},{5,4},{6,7},{7,6},{8,9},{9,8},{10,11... | collective-permute-start | bytes 614408 | tf_op jit(solution)/shard_map/cond/branch_6_fun/ppermute | solution.py:25
  23.6 9.4 %collective-permute-start.45 = (bf16[400,128]{1,0:T(8,128)(2,1)S(1)}, bf16[400,128]{1,0:T(8,128)(2,1)S(1)}, u32[]{:S(2)}, u32[]{:S(2)}) collective-permute-start(bf16[400,128]{1,0:T(8,128)(2,1)S(1)} %get-tuple-element.182), channel_id=1, source_target_pairs={{0,30},{1,31},{2,28},{3,29},{4,26},{5,27},{6,24},{7,25},{8,22},{9,... | collective-permute-start | bytes 307208 | tf_op jit(solution)/shard_map/cond/branch_6_fun/ppermute | solution.py:25
  26.7 8.0 %collective-permute-start.46 = (bf16[400,128]{1,0:T(8,128)(2,1)S(1)}, bf16[400,128]{1,0:T(8,128)(2,1)S(1)}, u32[]{:S(2)}, u32[]{:S(2)}) collective-permute-start(bf16[400,128]{1,0:T(8,128)(2,1)S(1)} %get-tuple-element.183), channel_id=1, source_target_pairs={{0,28},{1,29},{2,30},{3,31},{4,24},{5,25},{6,26},{7,27},{8,20},{9,... | collective-permute-start | bytes 307208 | tf_op jit(solution)/shard_map/cond/branch_6_fun/ppermute | solution.py:25
  28.3 6.4 %collective-permute-start.48 = (bf16[400,128]{1,0:T(8,128)(2,1)S(1)}, bf16[400,128]{1,0:T(8,128)(2,1)S(1)}, u32[]{:S(2)}, u32[]{:S(2)}) collective-permute-start(bf16[400,128]{1,0:T(8,128)(2,1)S(1)} %slice.212), channel_id=1, source_target_pairs={{0,2},{1,3},{2,0},{3,1},{4,6},{5,7},{6,4},{7,5},{8,10},{9,11},{10,... | collective-permute-start | bytes 307208 | tf_op jit(solution)/shard_map/cond/branch_6_fun/ppermute | solution.py:25
  34.9 13.7 %collective-permute-start.60 = (bf16[400,128]{1,0:T(8,128)(2,1)S(1)}, bf16[400,128]{1,0:T(8,128)(2,1)S(1)}, u32[]{:S(2)}, u32[]{:S(2)}) collective-permute-start(bf16[400,128]{1,0:T(8,128)(2,1)S(1)} %param.17), channel_id=1, source_target_pairs={{0,18},{1,19},{2,16},{3,17},{4,22},{5,23},{6,20},{7,21},{8,26},{9,... | collective-permute-start | bytes 307208 | tf_op jit(solution)/shard_map/cond/branch_3_fun/ppermute | solution.py:25
  40.5 8.8 %collective-permute-start.59 = (bf16[400,128]{1,0:T(8,128)(2,1)S(1)}, bf16[400,128]{1,0:T(8,128)(2,1)S(1)}, u32[]{:S(2)}, u32[]{:S(2)}) collective-permute-start(bf16[400,128]{1,0:T(8,128)(2,1)S(1)} %param.17), channel_id=1, source_target_pairs={{0,16},{1,17},{2,18},{3,19},{4,20},{5,21},{6,22},{7,23},{8,24},{9,... | collective-permute-start | bytes 307208 | tf_op jit(solution)/shard_map/cond/branch_3_fun/ppermute | solution.py:25
  40.5 8.8 %collective-permute-start.58 = (bf16[400,128]{1,0:T(8,128)(2,1)S(1)}, bf16[400,128]{1,0:T(8,128)(2,1)S(1)}, u32[]{:S(2)}, u32[]{:S(2)}) collective-permute-start(bf16[400,128]{1,0:T(8,128)(2,1)S(1)} %param.17), channel_id=1, source_target_pairs={{0,2},{1,3},{2,0},{3,1},{4,6},{5,7},{6,4},{7,5},{8,10},{9,11},{10,... | collective-permute-start | bytes 307208 | tf_op jit(solution)/shard_map/cond/branch_3_fun/ppermute | solution.py:25
  49.6 1.8 %collective-permute-start.100 = (bf16[400,512]{1,0:T(8,128)(2,1)S(1)}, bf16[400,512]{1,0:T(8,128)(2,1)S(1)}, u32[]{:S(2)}, u32[]{:S(2)}) collective-permute-start(bf16[400,512]{1,0:T(8,128)(2,1)S(1)} %get-tuple-element.282.held), channel_id=1, source_target_pairs={{0,1},{1,0},{2,3},{3,2},{4,5},{5,4},{6,7},{7,6},{8,9},{9,8},{10,11... | collective-permute-start | bytes 1228808 | tf_op jit(solution)/shard_map/ppermute | solution.py:25
  53.7 1.5 %collective-permute-start.101 = (bf16[400,256]{1,0:T(8,128)(2,1)S(1)}, bf16[400,256]{1,0:T(8,128)(2,1)S(1)}, u32[]{:S(2)}, u32[]{:S(2)}) collective-permute-start(bf16[400,256]{1,0:T(8,128)(2,1)S(1)} %get-tuple-element.268), channel_id=1, source_target_pairs={{0,1},{1,0},{2,3},{3,2},{4,5},{5,4},{6,7},{7,6},{8,9},{9,8},{10,11... | collective-permute-start | bytes 614408 | tf_op jit(solution)/shard_map/ppermute | solution.py:25
  55.4 3.9 %collective-permute-start.84 = (bf16[400,256]{1,0:T(8,128)(2,1)S(1)}, bf16[400,256]{1,0:T(8,128)(2,1)S(1)}, u32[]{:S(2)}, u32[]{:S(2)}) collective-permute-start(bf16[400,256]{1,0:T(8,128)(2,1)S(1)} %get-tuple-element.201), channel_id=1, source_target_pairs={{0,1},{1,0},{2,3},{3,2},{4,5},{5,4},{6,7},{7,6},{8,9},{9,8},{10,11... | collective-permute-start | bytes 614408 | tf_op jit(solution)/shard_map/cond/branch_3_fun/ppermute | solution.py:25
  55.6 9.9 %collective-permute-start.82 = (bf16[400,128]{1,0:T(8,128)(2,1)S(1)}, bf16[400,128]{1,0:T(8,128)(2,1)S(1)}, u32[]{:S(2)}, u32[]{:S(2)}) collective-permute-start(bf16[400,128]{1,0:T(8,128)(2,1)S(1)} %get-tuple-element.198), channel_id=1, source_target_pairs={{0,18},{1,19},{2,16},{3,17},{4,22},{5,23},{6,20},{7,21},{8,26},{9,... | collective-permute-start | bytes 307208 | tf_op jit(solution)/shard_map/cond/branch_3_fun/ppermute | solution.py:25
  55.9 11.1 %collective-permute-start.83 = (bf16[400,128]{1,0:T(8,128)(2,1)S(1)}, bf16[400,128]{1,0:T(8,128)(2,1)S(1)}, u32[]{:S(2)}, u32[]{:S(2)}) collective-permute-start(bf16[400,128]{1,0:T(8,128)(2,1)S(1)} %get-tuple-element.199), channel_id=1, source_target_pairs={{0,16},{1,17},{2,18},{3,19},{4,20},{5,21},{6,22},{7,23},{8,24},{9,... | collective-permute-start | bytes 307208 | tf_op jit(solution)/shard_map/cond/branch_3_fun/ppermute | solution.py:25
  59.4 7.6 %collective-permute-start.85 = (bf16[400,128]{1,0:T(8,128)(2,1)S(1)}, bf16[400,128]{1,0:T(8,128)(2,1)S(1)}, u32[]{:S(2)}, u32[]{:S(2)}) collective-permute-start(bf16[400,128]{1,0:T(8,128)(2,1)S(1)} %slice.216), channel_id=1, source_target_pairs={{0,2},{1,3},{2,0},{3,1},{4,6},{5,7},{6,4},{7,5},{8,10},{9,11},{10,... | collective-permute-start | bytes 307208 | tf_op jit(solution)/shard_map/cond/branch_3_fun/ppermute | solution.py:25
where the time goes:
time: 68.1 us; the launch traced here: 67.9 us
  waiting for transfers between devices  28 us (41%)
  starting transfers between devices  26 us (38%)
  Pallas kernels  10.2 us (15%)
  between operations  2.15 us (3%)
  local copies, waits for them, and re-layouts  0.84 us (1%)
    ppermute x18, waiting for transfers between devices, exchange(): return lax.ppermute(value, AXES, pairs)  28 us
    ppermute x18, starting transfers between devices, exchange(): return lax.ppermute(value, AXES, pairs)  26 us
    pallas_call x9, Pallas kernels, call(): pl.pallas_call(kernel, out_shape=[jax.ShapeDtypeStruct(*out) for out in o...  10.2 us
  transfers between devices with their start and end apart: 18, of which 10 were waited for; matrix products, arithmetic and copies ran while one was open for 0% of the time, Pallas kernels for 5%

commit v1 on v0

--- a/solution.py
+++ b/solution.py
@@ -138,7 +138,8 @@
         return (slot << (rows.bit_length() - 1)) | (ids & (rows - 1))
 
     def hot(ids, n):
-        return (lax.broadcasted_iota(jnp.int32, (n, ids.shape[1]), 0) == ids).astype(f32).astype(bf16)
+        match = lax.broadcasted_iota(jnp.int16, (n, ids.shape[1]), 0) == ids.astype(jnp.int16)
+        return jnp.where(match, jnp.ones((), bf16), jnp.zeros((), bf16))
 
     for side, hots in ((0, hot_lhs), (1, hot_rhs)):
         hots[:, :edges] = hot(place(ends[r, side]), 2 * half)
@@ -163,14 +164,14 @@
     counts,
     sent,
     kept,
-    grad_lhs,
-    grad_rhs,
-    rows_lhs,
     rows_rhs,
-    query_ref,
     back_ref,
     weight_rhs_ref,
     weight_lhs_ref,
+    weight_pos_ref,
+    grad_rhs,
+    rows_lhs,
+    query_ref,
 ):
     half = came.shape[1] // 2
     edges = rel_ref.shape[1]
@@ -207,12 +208,10 @@
         positive = jnp.sum(query * rhs, axis=0, keepdims=True)
         live = lax.broadcasted_iota(jnp.int32, (1, size), 1) + c * size < limit
         weight_pos = jnp.where(live, -sigmoid(-positive), 0.0)
-        grad_query = weight_pos * rhs + dot_nt(rows_rhs[:, drawn[c]], weight_rhs_ref[at[c]])
+        weight_pos_ref[:, at[c]] = weight_pos
         grad_back = dot_nt(rows_lhs[:, drawn[c]], weight_lhs_ref[at[c]])
-        grad_lhs[:, at[c]] = product(grad_query, conjugate(rel)).astype(bf16)
         grad_rhs[:, at[c]] = (weight_pos * query + product(grad_back, rel)).astype(bf16)
         grad_rhs[:, drawn[c]] = dot(query_ref[:, at[c]], weight_rhs_ref[at[c]]).astype(bf16)
-        grad_lhs[:, drawn[c]] = dot(back_ref[:, at[c]], weight_lhs_ref[at[c]]).astype(bf16)
 
     for c in range(blocks + 2):
         if c < blocks:
@@ -227,8 +226,21 @@
     kept[...] = dot_nt(grad_rhs[...], hot_rhs[:half]).astype(bf16)
 
 
-def own_kernel(grad_lhs, hot_lhs, sent, kept):
+def own_kernel(
+    blocks, rows_rhs, back, weight_rhs, weight_lhs, weight_pos, rel_ref, hot_lhs, sent, kept, grad_lhs
+):
     half = sent.shape[1]
+    edges = rel_ref.shape[1]
+    size = edges // blocks
+    negs = (hot_lhs.shape[1] - edges) // blocks
+    for c in range(blocks):
+        at = slice(c * size, (c + 1) * size)
+        drawn = slice(edges + c * negs, edges + (c + 1) * negs)
+        grad_query = weight_pos[:, at] * rows_rhs[:, at].astype(f32) + dot_nt(
+            rows_rhs[:, drawn], weight_rhs[at]
+        )
+        grad_lhs[:, at] = product(grad_query, conjugate(rel_ref[:, at].astype(f32))).astype(bf16)
+        grad_lhs[:, drawn] = dot(back[:, at], weight_lhs[at]).astype(bf16)
     sent[...] = dot_nt(grad_lhs[...], hot_lhs[half:]).astype(bf16)
     kept[...] = dot_nt(grad_lhs[...], hot_lhs[:half]).astype(bf16)
 
@@ -313,17 +325,24 @@
             2 * width * (drawn * part_rows + edges * relations.shape[1]),
         )
         pair = [((width, part_rows // 2), bf16)] * 2
-        sent, kept, grads = call(
+        sent, kept, *held_back = call(
             functools.partial(bucket_kernel, round_index, blocks),
-            pair + [((width, drawn), bf16)],
+            pair
+            + [((width, drawn), bf16), ((width, edges), bf16)]
+            + [((edges, negs), bf16)] * 2
+            + [((1, edges), f32)],
             (came, *prepared, edge_counts),
             2 * width * drawn * 3 * part_rows,
-            [pltpu.VMEM((width, drawn), bf16)] * 3
-            + [pltpu.VMEM((width, edges), bf16)] * 2
-            + [pltpu.VMEM((edges, negs), bf16)] * 2,
+            [pltpu.VMEM((width, drawn), bf16)] * 2 + [pltpu.VMEM((width, edges), bf16)],
         )
         came = exchange(sent, 0, 1)
-        sent_own, kept_own = call(own_kernel, pair, (grads, prepared[0]), 2 * width * drawn * part_rows)
+        sent_own, kept_own = call(
+            functools.partial(own_kernel, blocks),
+            pair,
+            (*held_back, prepared[2], prepared[0]),
+            2 * width * drawn * part_rows,
+            [pltpu.VMEM((width, drawn), bf16)],
+        )
         sums = kept.astype(f32) + came.astype(f32)
         near, far = (piece(sums, i, rows).astype(bf16) for i in range(2))
         total = returned(near, far, sent_own, kept_own, mask, field)

time: 68.1 us -> 67.6 us (level)
  transfers between devices with their start and end apart: 18 -> 18, of which waited for: 10 -> 11; matrix products, arithmetic and copies ran while one was open for 0% -> 0% of each run, Pallas kernels for 5% -> 5%
where the time goes in v1:
time: 67.6 us; the launch traced here: 67.4 us
  waiting for transfers between devices  28 us (41%)
  starting transfers between devices  25.9 us (38%)
  Pallas kernels  9.74 us (14%)
  between operations  2.13 us (3%)
  local copies, waits for them, and re-layouts  0.84 us (1%)
    ppermute x18, waiting for transfers between devices, exchange(): return lax.ppermute(value, AXES, pairs)  28 us
    ppermute x18, starting transfers between devices, exchange(): return lax.ppermute(value, AXES, pairs)  25.9 us
    pallas_call x9, Pallas kernels, call(): pl.pallas_call(kernel, out_shape=[jax.ShapeDtypeStruct(*out) for out in o...  9.74 us
  transfers between devices with their start and end apart: 18, of which 11 were waited for; matrix products, arithmetic and copies ran while one was open for 0% of the time, Pallas kernels for 5%

profile of v1, /device:TPU:0, one launch (start us, length us, event | category | flops | bytes accessed | tf_op | source)
XLA Modules:
  0.0 67.4 jit_solution(436801697176295485)
XLA Ops:
  0.6 1.2 %shard_map.95 = (bf16[400,128]{1,0:T(8,128)(2,1)S(1)}, s32[1]{0:T(128)}, s32[1]{0:T(128)}) custom-call(f32[400,128]{1,0:T(8,128)} %bitcast.7, s32[2]{0:T(128)} %plan.1), custom_call_target="tpu_custom_call" | custom-call | flops 1000 | bytes 1048576 | tf_op jit(solution)/shard_map/pallas_call | solution.py:277
  2.6 14.5 %conditional.4 = (bf16[400,512]{1,0:T(8,128)(2,1)S(1)}) conditional(s32[]{:T(128)} %bitcast.2, bf16[400,128]{1,0:T(8,128)(2,1)S(1)} %get-tuple-element.256, bf16[400,128]{1,0:T(8,128)(2,1)S(1)} %get-tuple-element.256, bf16[400,128]{1,0:T(8,128)(2,1)S(1)} %get-tuple-element.256, ...), branch_computations={%region_0.0_spmd, %region_1.0_spmd, %region_2.0_spmd, %region_3.0_... | conditional | flops 1638400 | bytes 2048128 | solution.py:52
  2.6 7.0 %collective-permute-start.20 = (bf16[400,128]{1,0:T(8,128)(2,1)S(1)}, bf16[400,128]{1,0:T(8,128)(2,1)S(1)}, u32[]{:S(2)}, u32[]{:S(2)}) collective-permute-start(bf16[400,128]{1,0:T(8,128)(2,1)S(1)} %param.6), channel_id=1, source_target_pairs={{0,30},{1,31},{2,28},{3,29},{4,26},{5,27},{6,24},{7,25},{8,22},{9,... | collective-permute-start | bytes 307208 | tf_op jit(solution)/shard_map/cond/branch_6_fun/ppermute | solution.py:25
  9.6 0.2 collective-permute-start.19
  9.8 0.5 collective-permute-start.18
  10.3 2.6 %collective-permute-done.20 = bf16[400,128]{1,0:T(8,128)(2,1)S(1)} collective-permute-done((bf16[400,128]{1,0:T(8,128)(2,1)S(1)}, bf16[400,128]{1,0:T(8,128)(2,1)S(1)}, u32[]{:S(2)}, u32[]{:S(2)}) %collective-permute-start.20) | collective-permute-done | bytes 102432 | tf_op jit(solution)/shard_map/cond/branch_6_fun/ppermute | solution.py:25
  12.9 4.1 %collective-permute-done.19 = bf16[400,128]{1,0:T(8,128)(2,1)S(1)} collective-permute-done((bf16[400,128]{1,0:T(8,128)(2,1)S(1)}, bf16[400,128]{1,0:T(8,128)(2,1)S(1)}, u32[]{:S(2)}, u32[]{:S(2)}) %collective-permute-start.19) | collective-permute-done | bytes 102432 | tf_op jit(solution)/shard_map/cond/branch_6_fun/ppermute | solution.py:25
  17.1 0.1 collective-permute-start.98
  17.1 0.1 copy.10.counts
  17.3 0.5 copy-done.4
  17.7 0.2 copy-done.5
  17.9 0.7 %shard_map.96 = (bf16[512,1024]{1,0:T(8,128)(2,1)S(1)}, bf16[512,1024]{1,0:T(8,128)(2,1)S(1)}, bf16[400,512]{1,0:T(8,128)(2,1)S(1)}, bf16[400,1024]{1,0:T(8,128)...) custom-call(bf16[400,512]{1,0:T(8,128)(2,1)S(1)} %get-tuple-element.296.held, ...), custom_call_target="tpu_custom_call" | custom-call | flops 524288000 | bytes 1048576 | tf_op jit(solution)/shard_map/pallas_call | solution.py:277
  18.7 0.2 collective-permute-done.98.came
  18.9 2.1 %shard_map.97 = (bf16[400,256]{1,0:T(8,128)(2,1)S(1)}, bf16[400,256]{1,0:T(8,128)(2,1)S(1)}, bf16[400,1024]{1,0:T(8,128)(2,1)S(1)}, bf16[400,512]{1,0:T(8,128)(2...) custom-call(bf16[400,512]{1,0:T(8,128)(2,1)S(1)} %collective-permute-done.98.came, ...), custom_call_target="tpu_custom_call" | custom-call | flops 1258291200 | bytes 1048576 | tf_op jit(solution)/shard_map/pallas_call | solution.py:277
  21.0 0.3 collective-permute-start.99
  22.0 0.9 %shard_map.98 = (bf16[400,256]{1,0:T(8,128)(2,1)S(1)}, bf16[400,256]{1,0:T(8,128)(2,1)S(1)}) custom-call(bf16[400,1024]{1,0:T(8,128)(2,1)S(1)} %get-tuple-element.264.rows_rhs, bf16[400,512]{1,0:T(8,128)(2,1)S(1)} %get-tuple-element.265.back, bf16[512,256]{1,0:T(8,128)(2,1)S(1)} %get-tuple-element.266.weight_rhs, ...), custom_call_target="tpu_custom_call" | custom-call | flops 419430400 | bytes 1048576 | tf_op jit(solution)/shard_map/pallas_call | solution.py:277
  22.9 0.1 add_convert_fusion.1
  23.0 11.5 %conditional.5 = (f32[400,128]{1,0:T(8,128)S(1)}) conditional(s32[]{:T(128)} %bitcast.2, (bf16[400,128]{1,0:T(8,128)(2,1)S(1)}, bf16[400,128]{1,0:T(8,128)(2,1)S(1)}, bf16[400,256]{1,0:T(8,128)(2,1)S(1)}, bf16[400,256]{1,0:T(8,128)(2,1)S(1)}) %tuple.92, (bf16[400,128]{1,0:T(8,128)(2,1)S(1)}, ...), branch_computations={%region_7.0_spmd, %region_8.0_spmd, %region_9.0_spmd, %region_10.0... | conditional | flops 614400 | bytes 3788968 | solution.py:52
  23.1 0.3 collective-permute-start.47
  23.4 3.2 %collective-permute-start.45 = (bf16[400,128]{1,0:T(8,128)(2,1)S(1)}, bf16[400,128]{1,0:T(8,128)(2,1)S(1)}, u32[]{:S(2)}, u32[]{:S(2)}) collective-permute-start(bf16[400,128]{1,0:T(8,128)(2,1)S(1)} %get-tuple-element.182), channel_id=1, source_target_pairs={{0,30},{1,31},{2,28},{3,29},{4,26},{5,27},{6,24},{7,25},{8,22},{9,... | collective-permute-start | bytes 307208 | tf_op jit(solution)/shard_map/cond/branch_6_fun/ppermute | solution.py:25
  26.5 1.5 %collective-permute-start.46 = (bf16[400,128]{1,0:T(8,128)(2,1)S(1)}, bf16[400,128]{1,0:T(8,128)(2,1)S(1)}, u32[]{:S(2)}, u32[]{:S(2)}) collective-permute-start(bf16[400,128]{1,0:T(8,128)(2,1)S(1)} %get-tuple-element.183), channel_id=1, source_target_pairs={{0,28},{1,29},{2,30},{3,31},{4,24},{5,25},{6,26},{7,27},{8,20},{9,... | collective-permute-start | bytes 307208 | tf_op jit(solution)/shard_map/cond/branch_6_fun/ppermute | solution.py:25
  28.2 1.6 %collective-permute-start.48 = (bf16[400,128]{1,0:T(8,128)(2,1)S(1)}, bf16[400,128]{1,0:T(8,128)(2,1)S(1)}, u32[]{:S(2)}, u32[]{:S(2)}) collective-permute-start(bf16[400,128]{1,0:T(8,128)(2,1)S(1)} %slice.212), channel_id=1, source_target_pairs={{0,2},{1,3},{2,0},{3,1},{4,6},{5,7},{6,4},{7,5},{8,10},{9,11},{10,... | collective-permute-start | bytes 307208 | tf_op jit(solution)/shard_map/cond/branch_6_fun/ppermute | solution.py:25
  29.7 3.0 %collective-permute-done.45 = bf16[400,128]{1,0:T(8,128)(2,1)S(1)} collective-permute-done((bf16[400,128]{1,0:T(8,128)(2,1)S(1)}, bf16[400,128]{1,0:T(8,128)(2,1)S(1)}, u32[]{:S(2)}, u32[]{:S(2)}) %collective-permute-start.45) | collective-permute-done | bytes 102432 | tf_op jit(solution)/shard_map/cond/branch_6_fun/ppermute | solution.py:25
  32.7 1.7 %collective-permute-done.46 = bf16[400,128]{1,0:T(8,128)(2,1)S(1)} collective-permute-done((bf16[400,128]{1,0:T(8,128)(2,1)S(1)}, bf16[400,128]{1,0:T(8,128)(2,1)S(1)}, u32[]{:S(2)}, u32[]{:S(2)}) %collective-permute-start.46) | collective-permute-done | bytes 102432 | tf_op jit(solution)/shard_map/cond/branch_6_fun/ppermute | solution.py:25
  34.4 0.1 fusion.6
  34.5 0.1 shard_map.99
  34.6 14.7 %conditional.6 = (bf16[400,512]{1,0:T(8,128)(2,1)S(1)}) conditional(s32[]{:T(128)} %bitcast.1, bf16[400,128]{1,0:T(8,128)(2,1)S(1)} %get-tuple-element.272, bf16[400,128]{1,0:T(8,128)(2,1)S(1)} %get-tuple-element.272, bf16[400,128]{1,0:T(8,128)(2,1)S(1)} %get-tuple-element.272, ...), branch_computations={%region_14.0_spmd, %region_15.0_spmd, %region_16.0_spmd, %region_1... | conditional | flops 1638400 | bytes 2048128 | solution.py:52
  34.6 5.7 %collective-permute-start.60 = (bf16[400,128]{1,0:T(8,128)(2,1)S(1)}, bf16[400,128]{1,0:T(8,128)(2,1)S(1)}, u32[]{:S(2)}, u32[]{:S(2)}) collective-permute-start(bf16[400,128]{1,0:T(8,128)(2,1)S(1)} %param.17), channel_id=1, source_target_pairs={{0,18},{1,19},{2,16},{3,17},{4,22},{5,23},{6,20},{7,21},{8,26},{9,... | collective-permute-start | bytes 307208 | tf_op jit(solution)/shard_map/cond/branch_3_fun/ppermute | solution.py:25
  40.3 0.6 collective-permute-start.58
  41.0 7.5 %collective-permute-done.60 = bf16[400,128]{1,0:T(8,128)(2,1)S(1)} collective-permute-done((bf16[400,128]{1,0:T(8,128)(2,1)S(1)}, bf16[400,128]{1,0:T(8,128)(2,1)S(1)}, u32[]{:S(2)}, u32[]{:S(2)}) %collective-permute-start.60) | collective-permute-done | bytes 102432 | tf_op jit(solution)/shard_map/cond/branch_3_fun/ppermute | solution.py:25
  48.4 0.7 collective-permute-done.59
  49.3 0.1 collective-permute-start.100
  49.4 0.8 %shard_map.100 = (bf16[512,1024]{1,0:T(8,128)(2,1)S(1)}, bf16[512,1024]{1,0:T(8,128)(2,1)S(1)}, bf16[400,512]{1,0:T(8,128)(2,1)S(1)}, bf16[400,1024]{1,0:T(8,128...) custom-call(bf16[400,512]{1,0:T(8,128)(2,1)S(1)} %get-tuple-element.298.held, ...), custom_call_target="tpu_custom_call" | custom-call | flops 524288000 | bytes 1048576 | tf_op jit(solution)/shard_map/pallas_call | solution.py:277
  50.2 1.0 %collective-permute-done.100.came = bf16[400,512]{1,0:T(8,128)(2,1)S(1)} collective-permute-done((bf16[400,512]{1,0:T(8,128)(2,1)S(1)}, bf16[400,512]{1,0:T(8,128)(2,1)S(1)}, u32[]{:S(2)}, u32[]{:S(2)}) %collective-permute-start.100) | collective-permute-done | bytes 409632 | tf_op jit(solution)/shard_map/ppermute | solution.py:25
  51.1 2.1 %shard_map.101 = (bf16[400,256]{1,0:T(8,128)(2,1)S(1)}, bf16[400,256]{1,0:T(8,128)(2,1)S(1)}, bf16[400,1024]{1,0:T(8,128)(2,1)S(1)}, bf16[400,512]{1,0:T(8,128)(...) custom-call(bf16[400,512]{1,0:T(8,128)(2,1)S(1)} %collective-permute-done.100.came, ...), custom_call_target="tpu_custom_call" | custom-call | flops 1258291200 | bytes 1048576 | tf_op jit(solution)/shard_map/pallas_call | solution.py:277
  53.3 0.2 collective-permute-start.101
  53.5 0.9 %shard_map.102 = (bf16[400,256]{1,0:T(8,128)(2,1)S(1)}, bf16[400,256]{1,0:T(8,128)(2,1)S(1)}) custom-call(bf16[400,1024]{1,0:T(8,128)(2,1)S(1)} %get-tuple-element.281.rows_rhs, bf16[400,512]{1,0:T(8,128)(2,1)S(1)} %get-tuple-element.282.back, bf16[512,256]{1,0:T(8,128)(2,1)S(1)} %get-tuple-element.283.weight_rhs, ...), custom_call_target="tpu_custom_call" | custom-call | flops 419430400 | bytes 1048576 | tf_op jit(solution)/shard_map/pallas_call | solution.py:277
  54.4 0.4 collective-permute-done.101
  54.8 0.1 add_convert_fusion
  54.9 11.8 %conditional.7 = (f32[400,128]{1,0:T(8,128)S(1)}) conditional(s32[]{:T(128)} %bitcast.1, (bf16[400,128]{1,0:T(8,128)(2,1)S(1)}, bf16[400,128]{1,0:T(8,128)(2,1)S(1)}, bf16[400,256]{1,0:T(8,128)(2,1)S(1)}, bf16[400,256]{1,0:T(8,128)(2,1)S(1)}) %tuple.93, (bf16[400,128]{1,0:T(8,128)(2,1)S(1)}, ...), branch_computations={%region_21.0_spmd, %region_22.0_spmd, %region_23.0_spmd, %region_2... | conditional | flops 614400 | bytes 3788968 | solution.py:52
  54.9 0.2 collective-permute-start.84
  55.1 0.4 collective-permute-start.82
  55.5 3.4 %collective-permute-start.83 = (bf16[400,128]{1,0:T(8,128)(2,1)S(1)}, bf16[400,128]{1,0:T(8,128)(2,1)S(1)}, u32[]{:S(2)}, u32[]{:S(2)}) collective-permute-start(bf16[400,128]{1,0:T(8,128)(2,1)S(1)} %get-tuple-element.199), channel_id=1, source_target_pairs={{0,16},{1,17},{2,18},{3,19},{4,20},{5,21},{6,22},{7,23},{8,24},{9,... | collective-permute-start | bytes 307208 | tf_op jit(solution)/shard_map/cond/branch_3_fun/ppermute | solution.py:25
  59.0 0.7 collective-permute-start.85
  59.7 5.3 %collective-permute-done.82 = bf16[400,128]{1,0:T(8,128)(2,1)S(1)} collective-permute-done((bf16[400,128]{1,0:T(8,128)(2,1)S(1)}, bf16[400,128]{1,0:T(8,128)(2,1)S(1)}, u32[]{:S(2)}, u32[]{:S(2)}) %collective-permute-start.82) | collective-permute-done | bytes 102432 | tf_op jit(solution)/shard_map/cond/branch_3_fun/ppermute | solution.py:25
  65.0 1.6 %collective-permute-done.83 = bf16[400,128]{1,0:T(8,128)(2,1)S(1)} collective-permute-done((bf16[400,128]{1,0:T(8,128)(2,1)S(1)}, bf16[400,128]{1,0:T(8,128)(2,1)S(1)}, u32[]{:S(2)}, u32[]{:S(2)}) %collective-permute-start.83) | collective-permute-done | bytes 102432 | tf_op jit(solution)/shard_map/cond/branch_3_fun/ppermute | solution.py:25
  66.6 0.1 fusion.10
  66.7 0.8 %shard_map.103 = (f32[400,128]{1,0:T(8,128)}, f32[1,128]{1,0:T(1,128)}) custom-call(f32[400,128]{1,0:T(8,128)S(1)} %get-tuple-element.299.total, f32[400,128]{1,0:T(8,128)S(1)} %get-tuple-element.288.rows, f32[1,128]{1,0:T(1,128)S(1)} %get-tuple-element.289.state), custom_call_target="tpu_custom_call" | custom-call | flops 1000 | bytes 1048576 | tf_op jit(solution)/shard_map/pallas_call | solution.py:277
  (28 shorter events, 0.3 us)
Async XLA Ops:
  2.5 14.6 %copy-start.6 = (s32[2,1,1]{0,2,1:T(1,128)S(1)}, s32[2,1,1]{0,2,1:T(1,128)}, u32[]{:S(2)}) copy-start(s32[2,1,1]{0,2,1:T(1,128)} %param.42) | copy-start | bytes 28
  2.5 14.7 %copy-start.1 = (bf16[256,400]{0,1:T(8,128)(2,1)S(1)}, bf16[256,400]{0,1:T(8,128)(2,1)}, u32[]{:S(2)}) copy-start(bf16[256,400]{0,1:T(8,128)(2,1)} %param.38) | copy-start | bytes 614404
  2.5 14.7 %copy-start.2 = (s32[2,2,1,512]{3,2,1,0:T(1,128)S(1)}, s32[2,2,1,512]{3,2,1,0:T(1,128)}, u32[]{:S(2)}) copy-start(s32[2,2,1,512]{3,2,1,0:T(1,128)} %ends.3) | copy-start | bytes 24580
  2.5 14.7 %copy-start.3 = (s32[2,2,1,2,256]{4,3,2,1,0:T(2,128)S(1)}, s32[2,2,1,2,256]{4,3,2,1,0:T(2,128)}, u32[]{:S(2)}) copy-start(s32[2,2,1,2,256]{4,3,2,1,0:T(2,128)} %negs.3) | copy-start | bytes 24580
  2.6 10.3 %collective-permute-start.20 = (bf16[400,128]{1,0:T(8,128)(2,1)S(1)}, bf16[400,128]{1,0:T(8,128)(2,1)S(1)}, u32[]{:S(2)}, u32[]{:S(2)}) collective-permute-start(bf16[400,128]{1,0:T(8,128)(2,1)S(1)} %param.6), channel_id=1, source_target_pairs={{0,30},{1,31},{2,28},{3,29},{4,26},{5,27},{6,24},{7,25},{8,22},{9,... | collective-permute-start | bytes 307208 | tf_op jit(solution)/shard_map/cond/branch_6_fun/ppermute | solution.py:25
  9.6 7.4 %collective-permute-start.19 = (bf16[400,128]{1,0:T(8,128)(2,1)S(1)}, bf16[400,128]{1,0:T(8,128)(2,1)S(1)}, u32[]{:S(2)}, u32[]{:S(2)}) collective-permute-start(bf16[400,128]{1,0:T(8,128)(2,1)S(1)} %param.6), channel_id=1, source_target_pairs={{0,28},{1,29},{2,30},{3,31},{4,24},{5,25},{6,26},{7,27},{8,20},{9,... | collective-permute-start | bytes 307208 | tf_op jit(solution)/shard_map/cond/branch_6_fun/ppermute | solution.py:25
  9.8 7.2 %collective-permute-start.18 = (bf16[400,128]{1,0:T(8,128)(2,1)S(1)}, bf16[400,128]{1,0:T(8,128)(2,1)S(1)}, u32[]{:S(2)}, u32[]{:S(2)}) collective-permute-start(bf16[400,128]{1,0:T(8,128)(2,1)S(1)} %param.6), channel_id=1, source_target_pairs={{0,2},{1,3},{2,0},{3,1},{4,6},{5,7},{6,4},{7,5},{8,10},{9,11},{10,... | collective-permute-start | bytes 307208 | tf_op jit(solution)/shard_map/cond/branch_6_fun/ppermute | solution.py:25
  17.0 0.7 %copy-start.4 = (s32[2,1,512]{2,1,0:T(1,128)S(1)}, s32[2,1,512]{2,1,0:T(1,128)}, u32[]{:S(2)}) copy-start(s32[2,1,512]{2,1,0:T(1,128)} %rels.3) | copy-start | bytes 12292
  17.1 1.8 %collective-permute-start.98 = (bf16[400,512]{1,0:T(8,128)(2,1)S(1)}, bf16[400,512]{1,0:T(8,128)(2,1)S(1)}, u32[]{:S(2)}, u32[]{:S(2)}) collective-permute-start(bf16[400,512]{1,0:T(8,128)(2,1)S(1)} %get-tuple-element.296.held), channel_id=1, source_target_pairs={{0,1},{1,0},{2,3},{3,2},{4,5},{5,4},{6,7},{7,6},{8,9},{9,8},{10,11... | collective-permute-start | bytes 1228808 | tf_op jit(solution)/shard_map/ppermute | solution.py:25
  17.2 0.7 copy-start.5
  21.0 1.9 %collective-permute-start.99 = (bf16[400,256]{1,0:T(8,128)(2,1)S(1)}, bf16[400,256]{1,0:T(8,128)(2,1)S(1)}, u32[]{:S(2)}, u32[]{:S(2)}) collective-permute-start(bf16[400,256]{1,0:T(8,128)(2,1)S(1)} %get-tuple-element.263), channel_id=1, source_target_pairs={{0,1},{1,0},{2,3},{3,2},{4,5},{5,4},{6,7},{7,6},{8,9},{9,8},{10,11... | collective-permute-start | bytes 614408 | tf_op jit(solution)/shard_map/ppermute | solution.py:25
  23.0 11.5 %copy-start = (f32[128,400]{0,1:T(8,128)S(1)}, f32[128,400]{0,1:T(8,128)}, u32[]{:S(2)}) copy-start(f32[128,400]{0,1:T(8,128)} %param.36) | copy-start | bytes 614404
  23.1 5.0 %collective-permute-start.47 = (bf16[400,256]{1,0:T(8,128)(2,1)S(1)}, bf16[400,256]{1,0:T(8,128)(2,1)S(1)}, u32[]{:S(2)}, u32[]{:S(2)}) collective-permute-start(bf16[400,256]{1,0:T(8,128)(2,1)S(1)} %get-tuple-element.185), channel_id=1, source_target_pairs={{0,1},{1,0},{2,3},{3,2},{4,5},{5,4},{6,7},{7,6},{8,9},{9,8},{10,11... | collective-permute-start | bytes 614408 | tf_op jit(solution)/shard_map/cond/branch_6_fun/ppermute | solution.py:25
  23.4 9.3 %collective-permute-start.45 = (bf16[400,128]{1,0:T(8,128)(2,1)S(1)}, bf16[400,128]{1,0:T(8,128)(2,1)S(1)}, u32[]{:S(2)}, u32[]{:S(2)}) collective-permute-start(bf16[400,128]{1,0:T(8,128)(2,1)S(1)} %get-tuple-element.182), channel_id=1, source_target_pairs={{0,30},{1,31},{2,28},{3,29},{4,26},{5,27},{6,24},{7,25},{8,22},{9,... | collective-permute-start | bytes 307208 | tf_op jit(solution)/shard_map/cond/branch_6_fun/ppermute | solution.py:25
  26.5 7.9 %collective-permute-start.46 = (bf16[400,128]{1,0:T(8,128)(2,1)S(1)}, bf16[400,128]{1,0:T(8,128)(2,1)S(1)}, u32[]{:S(2)}, u32[]{:S(2)}) collective-permute-start(bf16[400,128]{1,0:T(8,128)(2,1)S(1)} %get-tuple-element.183), channel_id=1, source_target_pairs={{0,28},{1,29},{2,30},{3,31},{4,24},{5,25},{6,26},{7,27},{8,20},{9,... | collective-permute-start | bytes 307208 | tf_op jit(solution)/shard_map/cond/branch_6_fun/ppermute | solution.py:25
  28.2 6.3 %collective-permute-start.48 = (bf16[400,128]{1,0:T(8,128)(2,1)S(1)}, bf16[400,128]{1,0:T(8,128)(2,1)S(1)}, u32[]{:S(2)}, u32[]{:S(2)}) collective-permute-start(bf16[400,128]{1,0:T(8,128)(2,1)S(1)} %slice.212), channel_id=1, source_target_pairs={{0,2},{1,3},{2,0},{3,1},{4,6},{5,7},{6,4},{7,5},{8,10},{9,11},{10,... | collective-permute-start | bytes 307208 | tf_op jit(solution)/shard_map/cond/branch_6_fun/ppermute | solution.py:25
  34.6 13.8 %collective-permute-start.60 = (bf16[400,128]{1,0:T(8,128)(2,1)S(1)}, bf16[400,128]{1,0:T(8,128)(2,1)S(1)}, u32[]{:S(2)}, u32[]{:S(2)}) collective-permute-start(bf16[400,128]{1,0:T(8,128)(2,1)S(1)} %param.17), channel_id=1, source_target_pairs={{0,18},{1,19},{2,16},{3,17},{4,22},{5,23},{6,20},{7,21},{8,26},{9,... | collective-permute-start | bytes 307208 | tf_op jit(solution)/shard_map/cond/branch_3_fun/ppermute | solution.py:25
  40.3 8.8 %collective-permute-start.59 = (bf16[400,128]{1,0:T(8,128)(2,1)S(1)}, bf16[400,128]{1,0:T(8,128)(2,1)S(1)}, u32[]{:S(2)}, u32[]{:S(2)}) collective-permute-start(bf16[400,128]{1,0:T(8,128)(2,1)S(1)} %param.17), channel_id=1, source_target_pairs={{0,16},{1,17},{2,18},{3,19},{4,20},{5,21},{6,22},{7,23},{8,24},{9,... | collective-permute-start | bytes 307208 | tf_op jit(solution)/shard_map/cond/branch_3_fun/ppermute | solution.py:25
  40.3 8.8 %collective-permute-start.58 = (bf16[400,128]{1,0:T(8,128)(2,1)S(1)}, bf16[400,128]{1,0:T(8,128)(2,1)S(1)}, u32[]{:S(2)}, u32[]{:S(2)}) collective-permute-start(bf16[400,128]{1,0:T(8,128)(2,1)S(1)} %param.17), channel_id=1, source_target_pairs={{0,2},{1,3},{2,0},{3,1},{4,6},{5,7},{6,4},{7,5},{8,10},{9,11},{10,... | collective-permute-start | bytes 307208 | tf_op jit(solution)/shard_map/cond/branch_3_fun/ppermute | solution.py:25
  49.3 1.8 %collective-permute-start.100 = (bf16[400,512]{1,0:T(8,128)(2,1)S(1)}, bf16[400,512]{1,0:T(8,128)(2,1)S(1)}, u32[]{:S(2)}, u32[]{:S(2)}) collective-permute-start(bf16[400,512]{1,0:T(8,128)(2,1)S(1)} %get-tuple-element.298.held), channel_id=1, source_target_pairs={{0,1},{1,0},{2,3},{3,2},{4,5},{5,4},{6,7},{7,6},{8,9},{9,8},{10,11... | collective-permute-start | bytes 1228808 | tf_op jit(solution)/shard_map/ppermute | solution.py:25
  53.3 1.5 %collective-permute-start.101 = (bf16[400,256]{1,0:T(8,128)(2,1)S(1)}, bf16[400,256]{1,0:T(8,128)(2,1)S(1)}, u32[]{:S(2)}, u32[]{:S(2)}) collective-permute-start(bf16[400,256]{1,0:T(8,128)(2,1)S(1)} %get-tuple-element.280), channel_id=1, source_target_pairs={{0,1},{1,0},{2,3},{3,2},{4,5},{5,4},{6,7},{7,6},{8,9},{9,8},{10,11... | collective-permute-start | bytes 614408 | tf_op jit(solution)/shard_map/ppermute | solution.py:25
  54.9 4.0 %collective-permute-start.84 = (bf16[400,256]{1,0:T(8,128)(2,1)S(1)}, bf16[400,256]{1,0:T(8,128)(2,1)S(1)}, u32[]{:S(2)}, u32[]{:S(2)}) collective-permute-start(bf16[400,256]{1,0:T(8,128)(2,1)S(1)} %get-tuple-element.201), channel_id=1, source_target_pairs={{0,1},{1,0},{2,3},{3,2},{4,5},{5,4},{6,7},{7,6},{8,9},{9,8},{10,11... | collective-permute-start | bytes 614408 | tf_op jit(solution)/shard_map/cond/branch_3_fun/ppermute | solution.py:25
  55.1 9.9 %collective-permute-start.82 = (bf16[400,128]{1,0:T(8,128)(2,1)S(1)}, bf16[400,128]{1,0:T(8,128)(2,1)S(1)}, u32[]{:S(2)}, u32[]{:S(2)}) collective-permute-start(bf16[400,128]{1,0:T(8,128)(2,1)S(1)} %get-tuple-element.198), channel_id=1, source_target_pairs={{0,18},{1,19},{2,16},{3,17},{4,22},{5,23},{6,20},{7,21},{8,26},{9,... | collective-permute-start | bytes 307208 | tf_op jit(solution)/shard_map/cond/branch_3_fun/ppermute | solution.py:25
  55.5 11.0 %collective-permute-start.83 = (bf16[400,128]{1,0:T(8,128)(2,1)S(1)}, bf16[400,128]{1,0:T(8,128)(2,1)S(1)}, u32[]{:S(2)}, u32[]{:S(2)}) collective-permute-start(bf16[400,128]{1,0:T(8,128)(2,1)S(1)} %get-tuple-element.199), channel_id=1, source_target_pairs={{0,16},{1,17},{2,18},{3,19},{4,20},{5,21},{6,22},{7,23},{8,24},{9,... | collective-permute-start | bytes 307208 | tf_op jit(solution)/shard_map/cond/branch_3_fun/ppermute | solution.py:25
  59.0 7.6 %collective-permute-start.85 = (bf16[400,128]{1,0:T(8,128)(2,1)S(1)}, bf16[400,128]{1,0:T(8,128)(2,1)S(1)}, u32[]{:S(2)}, u32[]{:S(2)}) collective-permute-start(bf16[400,128]{1,0:T(8,128)(2,1)S(1)} %slice.216), channel_id=1, source_target_pairs={{0,2},{1,3},{2,0},{3,1},{4,6},{5,7},{6,4},{7,5},{8,10},{9,11},{10,... | collective-permute-start | bytes 307208 | tf_op jit(solution)/shard_map/cond/branch_3_fun/ppermute | solution.py:25

commit v2 on v1

--- a/solution.py
+++ b/solution.py
@@ -213,15 +213,12 @@
         grad_rhs[:, at[c]] = (weight_pos * query + product(grad_back, rel)).astype(bf16)
         grad_rhs[:, drawn[c]] = dot(query_ref[:, at[c]], weight_rhs_ref[at[c]]).astype(bf16)
 
-    for c in range(blocks + 2):
-        if c < blocks:
-            gather(at[c])
-            gather(drawn[c])
-            products(c)
-        if 1 <= c <= blocks:
-            weights(c - 1)
-        if c >= 2:
-            grads(c - 2)
+    for c in range(blocks):
+        gather(at[c])
+        gather(drawn[c])
+    for step in (products, weights, grads):
+        for c in range(blocks):
+            step(c)
     sent[...] = dot_nt(grad_rhs[...], hot_rhs[half:]).astype(bf16)
     kept[...] = dot_nt(grad_rhs[...], hot_rhs[:half]).astype(bf16)
 

time: 67.6 us -> 67.6 us (level)
  no operation moved by 1% of the time
where the time goes in v2:
time: 67.6 us; the launch traced here: 67.4 us
  waiting for transfers between devices  28 us (41%)
  starting transfers between devices  25.9 us (38%)
  Pallas kernels  9.74 us (14%)
  between operations  2.13 us (3%)
  local copies, waits for them, and re-layouts  0.84 us (1%)
    ppermute x18, waiting for transfers between devices, exchange(): return lax.ppermute(value, AXES, pairs)  28 us
    ppermute x18, starting transfers between devices, exchange(): return lax.ppermute(value, AXES, pairs)  25.9 us
    pallas_call x9, Pallas kernels, call(): pl.pallas_call(kernel, out_shape=[jax.ShapeDtypeStruct(*out) for out in o...  9.74 us
  transfers between devices with their start and end apart: 18, of which 11 were waited for; matrix products, arithmetic and copies ran while one was open for 0% of the time, Pallas kernels for 5%

profile of v2, /device:TPU:0, one launch (start us, length us, event | category | flops | bytes accessed | tf_op | source)
XLA Modules:
  0.0 67.4 jit_solution(436801697176295485)
XLA Ops:
  0.6 1.2 %shard_map.95 = (bf16[400,128]{1,0:T(8,128)(2,1)S(1)}, s32[1]{0:T(128)}, s32[1]{0:T(128)}) custom-call(f32[400,128]{1,0:T(8,128)} %bitcast.7, s32[2]{0:T(128)} %plan.1), custom_call_target="tpu_custom_call" | custom-call | flops 1000 | bytes 1048576 | tf_op jit(solution)/shard_map/pallas_call | solution.py:274
  2.6 14.5 %conditional.4 = (bf16[400,512]{1,0:T(8,128)(2,1)S(1)}) conditional(s32[]{:T(128)} %bitcast.2, bf16[400,128]{1,0:T(8,128)(2,1)S(1)} %get-tuple-element.256, bf16[400,128]{1,0:T(8,128)(2,1)S(1)} %get-tuple-element.256, bf16[400,128]{1,0:T(8,128)(2,1)S(1)} %get-tuple-element.256, ...), branch_computations={%region_0.0_spmd, %region_1.0_spmd, %region_2.0_spmd, %region_3.0_... | conditional | flops 1638400 | bytes 2048128 | solution.py:52
  2.6 7.0 %collective-permute-start.20 = (bf16[400,128]{1,0:T(8,128)(2,1)S(1)}, bf16[400,128]{1,0:T(8,128)(2,1)S(1)}, u32[]{:S(2)}, u32[]{:S(2)}) collective-permute-start(bf16[400,128]{1,0:T(8,128)(2,1)S(1)} %param.6), channel_id=1, source_target_pairs={{0,30},{1,31},{2,28},{3,29},{4,26},{5,27},{6,24},{7,25},{8,22},{9,... | collective-permute-start | bytes 307208 | tf_op jit(solution)/shard_map/cond/branch_6_fun/ppermute | solution.py:25
  9.6 0.2 collective-permute-start.19
  9.8 0.5 collective-permute-start.18
  10.3 2.6 %collective-permute-done.20 = bf16[400,128]{1,0:T(8,128)(2,1)S(1)} collective-permute-done((bf16[400,128]{1,0:T(8,128)(2,1)S(1)}, bf16[400,128]{1,0:T(8,128)(2,1)S(1)}, u32[]{:S(2)}, u32[]{:S(2)}) %collective-permute-start.20) | collective-permute-done | bytes 102432 | tf_op jit(solution)/shard_map/cond/branch_6_fun/ppermute | solution.py:25
  12.9 4.1 %collective-permute-done.19 = bf16[400,128]{1,0:T(8,128)(2,1)S(1)} collective-permute-done((bf16[400,128]{1,0:T(8,128)(2,1)S(1)}, bf16[400,128]{1,0:T(8,128)(2,1)S(1)}, u32[]{:S(2)}, u32[]{:S(2)}) %collective-permute-start.19) | collective-permute-done | bytes 102432 | tf_op jit(solution)/shard_map/cond/branch_6_fun/ppermute | solution.py:25
  17.1 0.1 collective-permute-start.98
  17.1 0.1 copy.10.counts
  17.3 0.5 copy-done.4
  17.7 0.2 copy-done.5
  17.9 0.7 %shard_map.96 = (bf16[512,1024]{1,0:T(8,128)(2,1)S(1)}, bf16[512,1024]{1,0:T(8,128)(2,1)S(1)}, bf16[400,512]{1,0:T(8,128)(2,1)S(1)}, bf16[400,1024]{1,0:T(8,128)...) custom-call(bf16[400,512]{1,0:T(8,128)(2,1)S(1)} %get-tuple-element.296.held, ...), custom_call_target="tpu_custom_call" | custom-call | flops 524288000 | bytes 1048576 | tf_op jit(solution)/shard_map/pallas_call | solution.py:274
  18.7 0.2 collective-permute-done.98.came
  18.9 2.1 %shard_map.97 = (bf16[400,256]{1,0:T(8,128)(2,1)S(1)}, bf16[400,256]{1,0:T(8,128)(2,1)S(1)}, bf16[400,1024]{1,0:T(8,128)(2,1)S(1)}, bf16[400,512]{1,0:T(8,128)(2...) custom-call(bf16[400,512]{1,0:T(8,128)(2,1)S(1)} %collective-permute-done.98.came, ...), custom_call_target="tpu_custom_call" | custom-call | flops 1258291200 | bytes 1048576 | tf_op jit(solution)/shard_map/pallas_call | solution.py:274
  21.0 0.3 collective-permute-start.99
  22.0 0.9 %shard_map.98 = (bf16[400,256]{1,0:T(8,128)(2,1)S(1)}, bf16[400,256]{1,0:T(8,128)(2,1)S(1)}) custom-call(bf16[400,1024]{1,0:T(8,128)(2,1)S(1)} %get-tuple-element.264.rows_rhs, bf16[400,512]{1,0:T(8,128)(2,1)S(1)} %get-tuple-element.265.back, bf16[512,256]{1,0:T(8,128)(2,1)S(1)} %get-tuple-element.266.weight_rhs, ...), custom_call_target="tpu_custom_call" | custom-call | flops 419430400 | bytes 1048576 | tf_op jit(solution)/shard_map/pallas_call | solution.py:274
  22.9 0.1 add_convert_fusion.1
  23.0 11.5 %conditional.5 = (f32[400,128]{1,0:T(8,128)S(1)}) conditional(s32[]{:T(128)} %bitcast.2, (bf16[400,128]{1,0:T(8,128)(2,1)S(1)}, bf16[400,128]{1,0:T(8,128)(2,1)S(1)}, bf16[400,256]{1,0:T(8,128)(2,1)S(1)}, bf16[400,256]{1,0:T(8,128)(2,1)S(1)}) %tuple.92, (bf16[400,128]{1,0:T(8,128)(2,1)S(1)}, ...), branch_computations={%region_7.0_spmd, %region_8.0_spmd, %region_9.0_spmd, %region_10.0... | conditional | flops 614400 | bytes 3788968 | solution.py:52
  23.1 0.3 collective-permute-start.47
  23.4 3.2 %collective-permute-start.45 = (bf16[400,128]{1,0:T(8,128)(2,1)S(1)}, bf16[400,128]{1,0:T(8,128)(2,1)S(1)}, u32[]{:S(2)}, u32[]{:S(2)}) collective-permute-start(bf16[400,128]{1,0:T(8,128)(2,1)S(1)} %get-tuple-element.182), channel_id=1, source_target_pairs={{0,30},{1,31},{2,28},{3,29},{4,26},{5,27},{6,24},{7,25},{8,22},{9,... | collective-permute-start | bytes 307208 | tf_op jit(solution)/shard_map/cond/branch_6_fun/ppermute | solution.py:25
  26.5 1.5 %collective-permute-start.46 = (bf16[400,128]{1,0:T(8,128)(2,1)S(1)}, bf16[400,128]{1,0:T(8,128)(2,1)S(1)}, u32[]{:S(2)}, u32[]{:S(2)}) collective-permute-start(bf16[400,128]{1,0:T(8,128)(2,1)S(1)} %get-tuple-element.183), channel_id=1, source_target_pairs={{0,28},{1,29},{2,30},{3,31},{4,24},{5,25},{6,26},{7,27},{8,20},{9,... | collective-permute-start | bytes 307208 | tf_op jit(solution)/shard_map/cond/branch_6_fun/ppermute | solution.py:25
  28.2 1.6 %collective-permute-start.48 = (bf16[400,128]{1,0:T(8,128)(2,1)S(1)}, bf16[400,128]{1,0:T(8,128)(2,1)S(1)}, u32[]{:S(2)}, u32[]{:S(2)}) collective-permute-start(bf16[400,128]{1,0:T(8,128)(2,1)S(1)} %slice.212), channel_id=1, source_target_pairs={{0,2},{1,3},{2,0},{3,1},{4,6},{5,7},{6,4},{7,5},{8,10},{9,11},{10,... | collective-permute-start | bytes 307208 | tf_op jit(solution)/shard_map/cond/branch_6_fun/ppermute | solution.py:25
  29.7 3.0 %collective-permute-done.45 = bf16[400,128]{1,0:T(8,128)(2,1)S(1)} collective-permute-done((bf16[400,128]{1,0:T(8,128)(2,1)S(1)}, bf16[400,128]{1,0:T(8,128)(2,1)S(1)}, u32[]{:S(2)}, u32[]{:S(2)}) %collective-permute-start.45) | collective-permute-done | bytes 102432 | tf_op jit(solution)/shard_map/cond/branch_6_fun/ppermute | solution.py:25
  32.7 1.7 %collective-permute-done.46 = bf16[400,128]{1,0:T(8,128)(2,1)S(1)} collective-permute-done((bf16[400,128]{1,0:T(8,128)(2,1)S(1)}, bf16[400,128]{1,0:T(8,128)(2,1)S(1)}, u32[]{:S(2)}, u32[]{:S(2)}) %collective-permute-start.46) | collective-permute-done | bytes 102432 | tf_op jit(solution)/shard_map/cond/branch_6_fun/ppermute | solution.py:25
  34.4 0.1 fusion.6
  34.5 0.1 shard_map.99
  34.6 14.7 %conditional.6 = (bf16[400,512]{1,0:T(8,128)(2,1)S(1)}) conditional(s32[]{:T(128)} %bitcast.1, bf16[400,128]{1,0:T(8,128)(2,1)S(1)} %get-tuple-element.272, bf16[400,128]{1,0:T(8,128)(2,1)S(1)} %get-tuple-element.272, bf16[400,128]{1,0:T(8,128)(2,1)S(1)} %get-tuple-element.272, ...), branch_computations={%region_14.0_spmd, %region_15.0_spmd, %region_16.0_spmd, %region_1... | conditional | flops 1638400 | bytes 2048128 | solution.py:52
  34.6 5.7 %collective-permute-start.60 = (bf16[400,128]{1,0:T(8,128)(2,1)S(1)}, bf16[400,128]{1,0:T(8,128)(2,1)S(1)}, u32[]{:S(2)}, u32[]{:S(2)}) collective-permute-start(bf16[400,128]{1,0:T(8,128)(2,1)S(1)} %param.17), channel_id=1, source_target_pairs={{0,18},{1,19},{2,16},{3,17},{4,22},{5,23},{6,20},{7,21},{8,26},{9,... | collective-permute-start | bytes 307208 | tf_op jit(solution)/shard_map/cond/branch_3_fun/ppermute | solution.py:25
  40.3 0.6 collective-permute-start.58
  41.0 7.5 %collective-permute-done.60 = bf16[400,128]{1,0:T(8,128)(2,1)S(1)} collective-permute-done((bf16[400,128]{1,0:T(8,128)(2,1)S(1)}, bf16[400,128]{1,0:T(8,128)(2,1)S(1)}, u32[]{:S(2)}, u32[]{:S(2)}) %collective-permute-start.60) | collective-permute-done | bytes 102432 | tf_op jit(solution)/shard_map/cond/branch_3_fun/ppermute | solution.py:25
  48.4 0.7 collective-permute-done.59
  49.3 0.1 collective-permute-start.100
  49.4 0.8 %shard_map.100 = (bf16[512,1024]{1,0:T(8,128)(2,1)S(1)}, bf16[512,1024]{1,0:T(8,128)(2,1)S(1)}, bf16[400,512]{1,0:T(8,128)(2,1)S(1)}, bf16[400,1024]{1,0:T(8,128...) custom-call(bf16[400,512]{1,0:T(8,128)(2,1)S(1)} %get-tuple-element.298.held, ...), custom_call_target="tpu_custom_call" | custom-call | flops 524288000 | bytes 1048576 | tf_op jit(solution)/shard_map/pallas_call | solution.py:274
  50.2 1.0 %collective-permute-done.100.came = bf16[400,512]{1,0:T(8,128)(2,1)S(1)} collective-permute-done((bf16[400,512]{1,0:T(8,128)(2,1)S(1)}, bf16[400,512]{1,0:T(8,128)(2,1)S(1)}, u32[]{:S(2)}, u32[]{:S(2)}) %collective-permute-start.100) | collective-permute-done | bytes 409632 | tf_op jit(solution)/shard_map/ppermute | solution.py:25
  51.1 2.1 %shard_map.101 = (bf16[400,256]{1,0:T(8,128)(2,1)S(1)}, bf16[400,256]{1,0:T(8,128)(2,1)S(1)}, bf16[400,1024]{1,0:T(8,128)(2,1)S(1)}, bf16[400,512]{1,0:T(8,128)(...) custom-call(bf16[400,512]{1,0:T(8,128)(2,1)S(1)} %collective-permute-done.100.came, ...), custom_call_target="tpu_custom_call" | custom-call | flops 1258291200 | bytes 1048576 | tf_op jit(solution)/shard_map/pallas_call | solution.py:274
  53.3 0.2 collective-permute-start.101
  53.5 0.9 %shard_map.102 = (bf16[400,256]{1,0:T(8,128)(2,1)S(1)}, bf16[400,256]{1,0:T(8,128)(2,1)S(1)}) custom-call(bf16[400,1024]{1,0:T(8,128)(2,1)S(1)} %get-tuple-element.281.rows_rhs, bf16[400,512]{1,0:T(8,128)(2,1)S(1)} %get-tuple-element.282.back, bf16[512,256]{1,0:T(8,128)(2,1)S(1)} %get-tuple-element.283.weight_rhs, ...), custom_call_target="tpu_custom_call" | custom-call | flops 419430400 | bytes 1048576 | tf_op jit(solution)/shard_map/pallas_call | solution.py:274
  54.4 0.4 collective-permute-done.101
  54.8 0.1 add_convert_fusion
  54.9 11.8 %conditional.7 = (f32[400,128]{1,0:T(8,128)S(1)}) conditional(s32[]{:T(128)} %bitcast.1, (bf16[400,128]{1,0:T(8,128)(2,1)S(1)}, bf16[400,128]{1,0:T(8,128)(2,1)S(1)}, bf16[400,256]{1,0:T(8,128)(2,1)S(1)}, bf16[400,256]{1,0:T(8,128)(2,1)S(1)}) %tuple.93, (bf16[400,128]{1,0:T(8,128)(2,1)S(1)}, ...), branch_computations={%region_21.0_spmd, %region_22.0_spmd, %region_23.0_spmd, %region_2... | conditional | flops 614400 | bytes 3788968 | solution.py:52
  54.9 0.2 collective-permute-start.84
  55.1 0.4 collective-permute-start.82
  55.5 3.4 %collective-permute-start.83 = (bf16[400,128]{1,0:T(8,128)(2,1)S(1)}, bf16[400,128]{1,0:T(8,128)(2,1)S(1)}, u32[]{:S(2)}, u32[]{:S(2)}) collective-permute-start(bf16[400,128]{1,0:T(8,128)(2,1)S(1)} %get-tuple-element.199), channel_id=1, source_target_pairs={{0,16},{1,17},{2,18},{3,19},{4,20},{5,21},{6,22},{7,23},{8,24},{9,... | collective-permute-start | bytes 307208 | tf_op jit(solution)/shard_map/cond/branch_3_fun/ppermute | solution.py:25
  59.0 0.7 collective-permute-start.85
  59.7 5.3 %collective-permute-done.82 = bf16[400,128]{1,0:T(8,128)(2,1)S(1)} collective-permute-done((bf16[400,128]{1,0:T(8,128)(2,1)S(1)}, bf16[400,128]{1,0:T(8,128)(2,1)S(1)}, u32[]{:S(2)}, u32[]{:S(2)}) %collective-permute-start.82) | collective-permute-done | bytes 102432 | tf_op jit(solution)/shard_map/cond/branch_3_fun/ppermute | solution.py:25
  65.0 1.6 %collective-permute-done.83 = bf16[400,128]{1,0:T(8,128)(2,1)S(1)} collective-permute-done((bf16[400,128]{1,0:T(8,128)(2,1)S(1)}, bf16[400,128]{1,0:T(8,128)(2,1)S(1)}, u32[]{:S(2)}, u32[]{:S(2)}) %collective-permute-start.83) | collective-permute-done | bytes 102432 | tf_op jit(solution)/shard_map/cond/branch_3_fun/ppermute | solution.py:25
  66.6 0.1 fusion.10
  66.7 0.8 %shard_map.103 = (f32[400,128]{1,0:T(8,128)}, f32[1,128]{1,0:T(1,128)}) custom-call(f32[400,128]{1,0:T(8,128)S(1)} %get-tuple-element.299.total, f32[400,128]{1,0:T(8,128)S(1)} %get-tuple-element.288.rows, f32[1,128]{1,0:T(1,128)S(1)} %get-tuple-element.289.state), custom_call_target="tpu_custom_call" | custom-call | flops 1000 | bytes 1048576 | tf_op jit(solution)/shard_map/pallas_call | solution.py:274
  (28 shorter events, 0.3 us)
Async XLA Ops:
  2.5 14.6 %copy-start.6 = (s32[2,1,1]{0,2,1:T(1,128)S(1)}, s32[2,1,1]{0,2,1:T(1,128)}, u32[]{:S(2)}) copy-start(s32[2,1,1]{0,2,1:T(1,128)} %param.42) | copy-start | bytes 28
  2.5 14.7 %copy-start.1 = (bf16[256,400]{0,1:T(8,128)(2,1)S(1)}, bf16[256,400]{0,1:T(8,128)(2,1)}, u32[]{:S(2)}) copy-start(bf16[256,400]{0,1:T(8,128)(2,1)} %param.38) | copy-start | bytes 614404
  2.5 14.7 %copy-start.2 = (s32[2,2,1,512]{3,2,1,0:T(1,128)S(1)}, s32[2,2,1,512]{3,2,1,0:T(1,128)}, u32[]{:S(2)}) copy-start(s32[2,2,1,512]{3,2,1,0:T(1,128)} %ends.3) | copy-start | bytes 24580
  2.5 14.7 %copy-start.3 = (s32[2,2,1,2,256]{4,3,2,1,0:T(2,128)S(1)}, s32[2,2,1,2,256]{4,3,2,1,0:T(2,128)}, u32[]{:S(2)}) copy-start(s32[2,2,1,2,256]{4,3,2,1,0:T(2,128)} %negs.3) | copy-start | bytes 24580
  2.6 10.3 %collective-permute-start.20 = (bf16[400,128]{1,0:T(8,128)(2,1)S(1)}, bf16[400,128]{1,0:T(8,128)(2,1)S(1)}, u32[]{:S(2)}, u32[]{:S(2)}) collective-permute-start(bf16[400,128]{1,0:T(8,128)(2,1)S(1)} %param.6), channel_id=1, source_target_pairs={{0,30},{1,31},{2,28},{3,29},{4,26},{5,27},{6,24},{7,25},{8,22},{9,... | collective-permute-start | bytes 307208 | tf_op jit(solution)/shard_map/cond/branch_6_fun/ppermute | solution.py:25
  9.6 7.4 %collective-permute-start.19 = (bf16[400,128]{1,0:T(8,128)(2,1)S(1)}, bf16[400,128]{1,0:T(8,128)(2,1)S(1)}, u32[]{:S(2)}, u32[]{:S(2)}) collective-permute-start(bf16[400,128]{1,0:T(8,128)(2,1)S(1)} %param.6), channel_id=1, source_target_pairs={{0,28},{1,29},{2,30},{3,31},{4,24},{5,25},{6,26},{7,27},{8,20},{9,... | collective-permute-start | bytes 307208 | tf_op jit(solution)/shard_map/cond/branch_6_fun/ppermute | solution.py:25
  9.8 7.2 %collective-permute-start.18 = (bf16[400,128]{1,0:T(8,128)(2,1)S(1)}, bf16[400,128]{1,0:T(8,128)(2,1)S(1)}, u32[]{:S(2)}, u32[]{:S(2)}) collective-permute-start(bf16[400,128]{1,0:T(8,128)(2,1)S(1)} %param.6), channel_id=1, source_target_pairs={{0,2},{1,3},{2,0},{3,1},{4,6},{5,7},{6,4},{7,5},{8,10},{9,11},{10,... | collective-permute-start | bytes 307208 | tf_op jit(solution)/shard_map/cond/branch_6_fun/ppermute | solution.py:25
  17.0 0.7 %copy-start.4 = (s32[2,1,512]{2,1,0:T(1,128)S(1)}, s32[2,1,512]{2,1,0:T(1,128)}, u32[]{:S(2)}) copy-start(s32[2,1,512]{2,1,0:T(1,128)} %rels.3) | copy-start | bytes 12292
  17.1 1.8 %collective-permute-start.98 = (bf16[400,512]{1,0:T(8,128)(2,1)S(1)}, bf16[400,512]{1,0:T(8,128)(2,1)S(1)}, u32[]{:S(2)}, u32[]{:S(2)}) collective-permute-start(bf16[400,512]{1,0:T(8,128)(2,1)S(1)} %get-tuple-element.296.held), channel_id=1, source_target_pairs={{0,1},{1,0},{2,3},{3,2},{4,5},{5,4},{6,7},{7,6},{8,9},{9,8},{10,11... | collective-permute-start | bytes 1228808 | tf_op jit(solution)/shard_map/ppermute | solution.py:25
  17.2 0.7 copy-start.5
  21.0 1.9 %collective-permute-start.99 = (bf16[400,256]{1,0:T(8,128)(2,1)S(1)}, bf16[400,256]{1,0:T(8,128)(2,1)S(1)}, u32[]{:S(2)}, u32[]{:S(2)}) collective-permute-start(bf16[400,256]{1,0:T(8,128)(2,1)S(1)} %get-tuple-element.263), channel_id=1, source_target_pairs={{0,1},{1,0},{2,3},{3,2},{4,5},{5,4},{6,7},{7,6},{8,9},{9,8},{10,11... | collective-permute-start | bytes 614408 | tf_op jit(solution)/shard_map/ppermute | solution.py:25
  23.0 11.5 %copy-start = (f32[128,400]{0,1:T(8,128)S(1)}, f32[128,400]{0,1:T(8,128)}, u32[]{:S(2)}) copy-start(f32[128,400]{0,1:T(8,128)} %param.36) | copy-start | bytes 614404
  23.1 5.0 %collective-permute-start.47 = (bf16[400,256]{1,0:T(8,128)(2,1)S(1)}, bf16[400,256]{1,0:T(8,128)(2,1)S(1)}, u32[]{:S(2)}, u32[]{:S(2)}) collective-permute-start(bf16[400,256]{1,0:T(8,128)(2,1)S(1)} %get-tuple-element.185), channel_id=1, source_target_pairs={{0,1},{1,0},{2,3},{3,2},{4,5},{5,4},{6,7},{7,6},{8,9},{9,8},{10,11... | collective-permute-start | bytes 614408 | tf_op jit(solution)/shard_map/cond/branch_6_fun/ppermute | solution.py:25
  23.4 9.3 %collective-permute-start.45 = (bf16[400,128]{1,0:T(8,128)(2,1)S(1)}, bf16[400,128]{1,0:T(8,128)(2,1)S(1)}, u32[]{:S(2)}, u32[]{:S(2)}) collective-permute-start(bf16[400,128]{1,0:T(8,128)(2,1)S(1)} %get-tuple-element.182), channel_id=1, source_target_pairs={{0,30},{1,31},{2,28},{3,29},{4,26},{5,27},{6,24},{7,25},{8,22},{9,... | collective-permute-start | bytes 307208 | tf_op jit(solution)/shard_map/cond/branch_6_fun/ppermute | solution.py:25
  26.5 7.9 %collective-permute-start.46 = (bf16[400,128]{1,0:T(8,128)(2,1)S(1)}, bf16[400,128]{1,0:T(8,128)(2,1)S(1)}, u32[]{:S(2)}, u32[]{:S(2)}) collective-permute-start(bf16[400,128]{1,0:T(8,128)(2,1)S(1)} %get-tuple-element.183), channel_id=1, source_target_pairs={{0,28},{1,29},{2,30},{3,31},{4,24},{5,25},{6,26},{7,27},{8,20},{9,... | collective-permute-start | bytes 307208 | tf_op jit(solution)/shard_map/cond/branch_6_fun/ppermute | solution.py:25
  28.2 6.3 %collective-permute-start.48 = (bf16[400,128]{1,0:T(8,128)(2,1)S(1)}, bf16[400,128]{1,0:T(8,128)(2,1)S(1)}, u32[]{:S(2)}, u32[]{:S(2)}) collective-permute-start(bf16[400,128]{1,0:T(8,128)(2,1)S(1)} %slice.212), channel_id=1, source_target_pairs={{0,2},{1,3},{2,0},{3,1},{4,6},{5,7},{6,4},{7,5},{8,10},{9,11},{10,... | collective-permute-start | bytes 307208 | tf_op jit(solution)/shard_map/cond/branch_6_fun/ppermute | solution.py:25
  34.6 13.8 %collective-permute-start.60 = (bf16[400,128]{1,0:T(8,128)(2,1)S(1)}, bf16[400,128]{1,0:T(8,128)(2,1)S(1)}, u32[]{:S(2)}, u32[]{:S(2)}) collective-permute-start(bf16[400,128]{1,0:T(8,128)(2,1)S(1)} %param.17), channel_id=1, source_target_pairs={{0,18},{1,19},{2,16},{3,17},{4,22},{5,23},{6,20},{7,21},{8,26},{9,... | collective-permute-start | bytes 307208 | tf_op jit(solution)/shard_map/cond/branch_3_fun/ppermute | solution.py:25
  40.3 8.8 %collective-permute-start.59 = (bf16[400,128]{1,0:T(8,128)(2,1)S(1)}, bf16[400,128]{1,0:T(8,128)(2,1)S(1)}, u32[]{:S(2)}, u32[]{:S(2)}) collective-permute-start(bf16[400,128]{1,0:T(8,128)(2,1)S(1)} %param.17), channel_id=1, source_target_pairs={{0,16},{1,17},{2,18},{3,19},{4,20},{5,21},{6,22},{7,23},{8,24},{9,... | collective-permute-start | bytes 307208 | tf_op jit(solution)/shard_map/cond/branch_3_fun/ppermute | solution.py:25
  40.3 8.8 %collective-permute-start.58 = (bf16[400,128]{1,0:T(8,128)(2,1)S(1)}, bf16[400,128]{1,0:T(8,128)(2,1)S(1)}, u32[]{:S(2)}, u32[]{:S(2)}) collective-permute-start(bf16[400,128]{1,0:T(8,128)(2,1)S(1)} %param.17), channel_id=1, source_target_pairs={{0,2},{1,3},{2,0},{3,1},{4,6},{5,7},{6,4},{7,5},{8,10},{9,11},{10,... | collective-permute-start | bytes 307208 | tf_op jit(solution)/shard_map/cond/branch_3_fun/ppermute | solution.py:25
  49.3 1.8 %collective-permute-start.100 = (bf16[400,512]{1,0:T(8,128)(2,1)S(1)}, bf16[400,512]{1,0:T(8,128)(2,1)S(1)}, u32[]{:S(2)}, u32[]{:S(2)}) collective-permute-start(bf16[400,512]{1,0:T(8,128)(2,1)S(1)} %get-tuple-element.298.held), channel_id=1, source_target_pairs={{0,1},{1,0},{2,3},{3,2},{4,5},{5,4},{6,7},{7,6},{8,9},{9,8},{10,11... | collective-permute-start | bytes 1228808 | tf_op jit(solution)/shard_map/ppermute | solution.py:25
  53.3 1.5 %collective-permute-start.101 = (bf16[400,256]{1,0:T(8,128)(2,1)S(1)}, bf16[400,256]{1,0:T(8,128)(2,1)S(1)}, u32[]{:S(2)}, u32[]{:S(2)}) collective-permute-start(bf16[400,256]{1,0:T(8,128)(2,1)S(1)} %get-tuple-element.280), channel_id=1, source_target_pairs={{0,1},{1,0},{2,3},{3,2},{4,5},{5,4},{6,7},{7,6},{8,9},{9,8},{10,11... | collective-permute-start | bytes 614408 | tf_op jit(solution)/shard_map/ppermute | solution.py:25
  54.9 4.0 %collective-permute-start.84 = (bf16[400,256]{1,0:T(8,128)(2,1)S(1)}, bf16[400,256]{1,0:T(8,128)(2,1)S(1)}, u32[]{:S(2)}, u32[]{:S(2)}) collective-permute-start(bf16[400,256]{1,0:T(8,128)(2,1)S(1)} %get-tuple-element.201), channel_id=1, source_target_pairs={{0,1},{1,0},{2,3},{3,2},{4,5},{5,4},{6,7},{7,6},{8,9},{9,8},{10,11... | collective-permute-start | bytes 614408 | tf_op jit(solution)/shard_map/cond/branch_3_fun/ppermute | solution.py:25
  55.1 9.9 %collective-permute-start.82 = (bf16[400,128]{1,0:T(8,128)(2,1)S(1)}, bf16[400,128]{1,0:T(8,128)(2,1)S(1)}, u32[]{:S(2)}, u32[]{:S(2)}) collective-permute-start(bf16[400,128]{1,0:T(8,128)(2,1)S(1)} %get-tuple-element.198), channel_id=1, source_target_pairs={{0,18},{1,19},{2,16},{3,17},{4,22},{5,23},{6,20},{7,21},{8,26},{9,... | collective-permute-start | bytes 307208 | tf_op jit(solution)/shard_map/cond/branch_3_fun/ppermute | solution.py:25
  55.5 11.0 %collective-permute-start.83 = (bf16[400,128]{1,0:T(8,128)(2,1)S(1)}, bf16[400,128]{1,0:T(8,128)(2,1)S(1)}, u32[]{:S(2)}, u32[]{:S(2)}) collective-permute-start(bf16[400,128]{1,0:T(8,128)(2,1)S(1)} %get-tuple-element.199), channel_id=1, source_target_pairs={{0,16},{1,17},{2,18},{3,19},{4,20},{5,21},{6,22},{7,23},{8,24},{9,... | collective-permute-start | bytes 307208 | tf_op jit(solution)/shard_map/cond/branch_3_fun/ppermute | solution.py:25
  59.0 7.6 %collective-permute-start.85 = (bf16[400,128]{1,0:T(8,128)(2,1)S(1)}, bf16[400,128]{1,0:T(8,128)(2,1)S(1)}, u32[]{:S(2)}, u32[]{:S(2)}) collective-permute-start(bf16[400,128]{1,0:T(8,128)(2,1)S(1)} %slice.216), channel_id=1, source_target_pairs={{0,2},{1,3},{2,0},{3,1},{4,6},{5,7},{6,4},{7,5},{8,10},{9,11},{10,... | collective-permute-start | bytes 307208 | tf_op jit(solution)/shard_map/cond/branch_3_fun/ppermute | solution.py:25
